TPU v7x, 256 devices: a whole 4x4x8 slice. The times are simulated.
256 devices in a mesh: rows: 16 (over z_lo, x), cols: 16 (over y, z_hi, core).
Axes of the slice: x: 4, y: 4, z: 8 (z_hi: 2, z_lo: 4; z = z_hi * 4 + z_lo), core: 2. Of those that a mesh axis runs over, the one named last changes fastest.
Arguments:
- kernel_hat: bfloat16 [2, 256, 512, 4096], P(None, 'rows', 'cols'), may hold values from -0.5 to 0.5
- coefficients: float32 [128, 512], P(None, 'cols'), may hold values from -6 to 6
- wave_speed_sq: float32 [4096, 4096], P('rows', 'cols'), may hold values from 1 to 4
- wet_mask: int32 [4096, 4096], P('rows', 'cols'), may hold values 0 or 1
- boundary_cell: int32 [4096], replicated, may hold values from 0 to 4095, each once
- height: float32 [4096, 4096], P('rows', 'cols'), may hold values from -3 to 3
- flux_x: float32 [4096, 4096], P('rows', 'cols'), may hold values from -3 to 3
- flux_y: float32 [4096, 4096], P('rows', 'cols'), may hold values from -3 to 3
Outputs:
- boundary_series: float32 [128, 4096], P('rows', 'cols')
- height_out: float32 [4096, 4096], P('rows', 'cols')
- flux_x_out: float32 [4096, 4096], P('rows', 'cols')
- flux_y_out: float32 [4096, 4096], P('rows', 'cols')
Inputs may be any that keep to these rules, and one draw needn't show every extreme that they name: `boundary_cell`: each of the 4096 boundary points names a different grid column, so each column is named by exactly one point.
All inputs are finite; a program needn't handle non-finite values. No bound on the sum of `wet_mask` on one device may be relied on, other than what follows from the above.
Results may differ from a plain program's by a relative error of at most 0.0029.
Values sent between devices are 32-bit elements; how exact they have to be, the bound alone decides.
A program may use at most 64 MiB of HBM per device.

v0:
```python
import math

import jax
import jax.numpy as jnp
from jax import lax
from jax.sharding import PartitionSpec as P

STEP_RATIO = 0.25


def split_up(x, dim, length):
    lengths = x.shape
    tiles = x.reshape(*lengths[:dim], length, lengths[dim] // length, *lengths[dim + 1 :])
    return jnp.moveaxis(tiles, dim, 0)


def summed_on_arrival(x, axis, dim):
    length = lax.axis_size(axis)
    tiles = lax.all_to_all(split_up(x, dim, length), axis, 0, 0, tiled=True)
    return jnp.sum(tiles, axis=0)


def copy_for_each(x, axis):
    copies = jnp.broadcast_to(x, (lax.axis_size(axis), *x.shape))
    return lax.all_to_all(copies, axis, split_axis=0, concat_axis=0, tiled=True)


def joined_along(tiles, dim):
    lengths = list(tiles.shape[1:])
    lengths[dim] *= tiles.shape[0]
    return jnp.moveaxis(tiles, 0, dim).reshape(lengths)


def gathered_copies(x, axis, dim):
    tiles = copy_for_each(x, axis)
    return joined_along(tiles, dim)


def with_halo(cells, sides, width):
    for axis, dim in sides:
        count = lax.axis_size(axis)
        ends = count - 1
        head = lax.slice_in_dim(cells, 0, width, axis=dim)
        tail = lax.slice_in_dim(cells, cells.shape[dim] - width, cells.shape[dim], axis=dim)
        cells = jnp.concatenate(
            [
                lax.ppermute(tail, axis, [(i, (i + 1) % count) for i in range(ends)]),
                cells,
                lax.ppermute(head, axis, [((i + 1) % count, i) for i in range(ends)]),
            ],
            axis=dim,
        )
    return cells


def neighbours(values, along_dim):
    if along_dim == 1:
        return (values[1:-1, :-1], values[1:-1, 1:])
    return (values[:-1, 1:-1], values[1:, 1:-1])


def face_fluxes(surface, along, across, speed_sq, celerity, wet, along_dim):
    left_surf, right_surf = neighbours(surface, along_dim)
    left_along, right_along = neighbours(along, along_dim)
    left_across, right_across = neighbours(across, along_dim)
    left_sq, right_sq = neighbours(speed_sq, along_dim)
    left_speed, right_speed = neighbours(celerity, along_dim)
    left_wet, right_wet = neighbours(wet, along_dim)
    opened = left_wet * right_wet
    damping = 0.25 * (left_speed + right_speed)
    mass_flux = opened * (0.5 * (left_along + right_along) - damping * (right_surf - left_surf))
    momentum = opened * (
        0.5 * (left_sq * left_surf + right_sq * right_surf) - damping * (right_along - left_along)
    )
    shear_flux = opened * (-damping * (right_across - left_across))
    return (mass_flux, momentum, shear_flux)


def advance(surface, along_x, along_y, speed_sq, wet):
    celerity = jnp.sqrt(speed_sq)
    mass_x, momentum_x, shear_x = face_fluxes(surface, along_x, along_y, speed_sq, celerity, wet, 1)
    mass_y, momentum_y, shear_y = face_fluxes(surface, along_y, along_x, speed_sq, celerity, wet, 0)
    interior_wet = wet[1:-1, 1:-1]

    def update(values, flux_cols, flux_rows):
        change = flux_cols[:, 1:] - flux_cols[:, :-1] + (flux_rows[1:] - flux_rows[:-1])
        return interior_wet * (values[1:-1, 1:-1] - STEP_RATIO * change)

    return (
        update(surface, mass_x, mass_y),
        update(along_x, momentum_x, shear_y),
        update(along_y, shear_x, momentum_y),
    )


def set_row(values, position, replacement, flag):
    return values.at[position].set(jnp.where(flag, replacement, values[position]))


def on_device(
    kernel_hat, coefficients, wave_speed_sq, wet_mask, boundary_cell, height, flux_x, flux_y
):
    high = lax.Precision.HIGHEST
    freq_dev = kernel_hat.shape[1]
    steps_total = coefficients.shape[0]
    freq_total = freq_dev * lax.axis_size("rows")
    freqs = lax.axis_index("rows") * freq_dev + jnp.arange(freq_dev, dtype=jnp.int32)
    times = jnp.arange(steps_total, dtype=jnp.int32)
    factor = 2.0 * math.pi / freq_total
    forward = (freqs[:, None] * times[None, :] % freq_total).astype(jnp.float32) * factor
    coef_re = jnp.dot(jnp.cos(forward), coefficients, precision=high).astype(jnp.bfloat16)
    coef_im = (-jnp.dot(jnp.sin(forward), coefficients, precision=high)).astype(jnp.bfloat16)
    form = "fso,fs->fo"
    kern_re = kernel_hat[0]
    kern_im = kernel_hat[1]
    spec_re = jnp.einsum(form, kern_re, coef_re, preferred_element_type=jnp.float32) - jnp.einsum(
        form, kern_im, coef_im, preferred_element_type=jnp.float32
    )
    spec_im = jnp.einsum(form, kern_re, coef_im, preferred_element_type=jnp.float32) + jnp.einsum(
        form, kern_im, coef_re, preferred_element_type=jnp.float32
    )
    inverse = (times[:, None] * freqs[None, :] % freq_total).astype(jnp.float32) * factor
    inv_cos = jnp.cos(inverse) / freq_total
    inv_sin = jnp.sin(inverse) / freq_total
    summed = summed_on_arrival(jnp.stack([spec_re, spec_im]), "cols", 2)
    partial_value = jnp.dot(inv_cos, summed[0], precision=high) - jnp.dot(
        inv_sin, summed[1], precision=high
    )
    series = summed_on_arrival(partial_value, "rows", 0)
    latest = gathered_copies(series[-2:], "cols", 1)
    tile_width = height.shape[1]
    columns = lax.axis_index("cols") * tile_width - 2 + jnp.arange(tile_width + 4, dtype=jnp.int32)
    selector = (boundary_cell[:, None] == columns[None, :]).astype(jnp.float32)
    ghost_wide = jnp.dot(latest, selector, precision=high)
    at_edge = lax.axis_index("rows") == lax.axis_size("rows") - 1
    wet = wet_mask.astype(jnp.float32)
    speed_pad, wet_pad = (
        with_halo(wave_speed_sq, (("rows", 0), ("cols", 1)), 2),
        with_halo(wet, (("rows", 0), ("cols", 1)), 2),
    )
    speed_pad = set_row(speed_pad, -2, 1.0, at_edge)
    wet_pad = set_row(wet_pad, -2, 1.0, at_edge)
    surf_pad, pad_x, pad_y = (
        with_halo(height, (("rows", 0), ("cols", 1)), 2),
        with_halo(flux_x, (("rows", 0), ("cols", 1)), 2),
        with_halo(flux_y, (("rows", 0), ("cols", 1)), 2),
    )
    surf_pad = set_row(surf_pad, -2, ghost_wide[0], at_edge)
    surface, along_x, along_y = advance(surf_pad, pad_x, pad_y, speed_pad, wet_pad)
    surface = set_row(surface, -1, ghost_wide[1, 1:-1], at_edge)
    along_x = set_row(along_x, -1, 0.0, at_edge)
    along_y = set_row(along_y, -1, 0.0, at_edge)
    surface, along_x, along_y = advance(
        surface, along_x, along_y, speed_pad[1:-1, 1:-1], wet_pad[1:-1, 1:-1]
    )
    return (series, surface, along_x, along_y)


def solution(mesh):
    return jax.shard_map(
        on_device,
        mesh=mesh,
        in_specs=(
            P(None, "rows", "cols", None),
            P(None, "cols"),
            P("rows", "cols"),
            P("rows", "cols"),
            P(),
            P("rows", "cols"),
            P("rows", "cols"),
            P("rows", "cols"),
        ),
        out_specs=(P("rows", "cols"), P("rows", "cols"), P("rows", "cols"), P("rows", "cols")),
        check_vma=False,
    )
```

profile of v0, /device:TPU:1, one launch (start us, length us, event | category | flops | bytes accessed | tf_op | source)
XLA Modules:
  0.0 173.3 jit_solution(15571838280219336880)
XLA Ops:
  0.7 0.7 copy-done
  1.9 3.0 %fusion.8 = f32[16,1,4096]{2,1,0:T(1,128)S(1)} fusion(bf16[2,16,32,4096]{3,2,1,0:T(8,128)(2,1)} %param.20, bf16[16,32,1]{1,0,2:T(8,128)(2,1)S(1)} %fusion.18), kind=kOutput, calls=%fused_computation.8 | convolution fusion | flops 4194304 | bytes 4457472 | tf_op jit(solution)/shard_map/fso,fs->fo/dot_general | solution.py:116
  4.9 3.4 %fusion.2 = f32[16,1,4096]{2,1,0:T(1,128)S(1)} fusion(bf16[2,16,32,4096]{3,2,1,0:T(8,128)(2,1)} %param.20, bf16[16,32,1]{1,0,2:T(8,128)(2,1)S(1)} %fusion.18), kind=kOutput, calls=%fused_computation.2 | convolution fusion | flops 4194304 | bytes 4457472 | tf_op jit(solution)/shard_map/fso,fs->fo/dot_general | solution.py:119
  10.4 1.1 copy.13
  11.6 12.6 %all-to-all-start = ((f32[16,2,16,256]{3,2,1,0:T(8,128)}), f32[16,2,16,256]{3,2,1,0:T(8,128)S(1)}, u32[]{:S(2)}, u32[]{:S(2)}) async-start(f32[16,2,16,256]{3,2,1,0:T(8,128)} %copy.13), calls=%async_computation | async-start | bytes 1048576 | tf_op jit(solution)/shard_map/all_to_all | solution.py:19
  24.2 3.1 %collective-permute-start.4 = (f32[2,256]{1,0:T(2,128)S(1)}, f32[2,256]{1,0:T(2,128)S(1)}, u32[]{:S(2)}, u32[]{:S(2)}) collective-permute-start(f32[2,256]{1,0:T(2,128)S(1)} %get-tuple-element.108), channel_id=1, source_target_pairs={{0,16},{16,32},{32,48},{48,64},{64,80},{80,96},{96,112},{112,128},... | collective-permute-start | bytes 6152 | tf_op jit(solution)/shard_map/ppermute | solution.py:47
  27.3 1.3 collective-permute-start.5
  28.6 4.0 %collective-permute-start = (f32[2,256]{1,0:T(2,128)S(1)}, f32[2,256]{1,0:T(2,128)S(1)}, u32[]{:S(2)}, u32[]{:S(2)}) collective-permute-start(f32[2,256]{1,0:T(2,128)S(1)} %get-tuple-element.104), channel_id=1, source_target_pairs={{0,16},{16,32},{32,48},{48,64},{64,80},{80,96},{96,112},{112,128},... | collective-permute-start | bytes 6152 | tf_op jit(solution)/shard_map/ppermute | solution.py:47
  32.6 1.3 collective-permute-start.1
  34.0 4.0 %collective-permute-start.12 = (f32[2,256]{1,0:T(2,128)S(1)}, f32[2,256]{1,0:T(2,128)S(1)}, u32[]{:S(2)}, u32[]{:S(2)}) collective-permute-start(f32[2,256]{1,0:T(2,128)S(1)} %get-tuple-element.102), channel_id=1, source_target_pairs={{0,16},{16,32},{32,48},{48,64},{64,80},{80,96},{96,112},{112,128},... | collective-permute-start | bytes 6152 | tf_op jit(solution)/shard_map/ppermute | solution.py:47
  38.0 1.3 collective-permute-start.13
  39.3 4.0 %collective-permute-start.16 = (f32[2,256]{1,0:T(2,128)S(1)}, f32[2,256]{1,0:T(2,128)S(1)}, u32[]{:S(2)}, u32[]{:S(2)}) collective-permute-start(f32[2,256]{1,0:T(2,128)S(1)} %get-tuple-element.106), channel_id=1, source_target_pairs={{0,16},{16,32},{32,48},{48,64},{64,80},{80,96},{96,112},{112,128},... | collective-permute-start | bytes 6152 | tf_op jit(solution)/shard_map/ppermute | solution.py:47
  43.4 0.8 fusion.123
  44.1 1.3 collective-permute-start.17
  45.4 4.5 %collective-permute-start.8 = (f32[2,256]{1,0:T(2,128)S(1)}, f32[2,256]{1,0:T(2,128)S(1)}, u32[]{:S(2)}, u32[]{:S(2)}) collective-permute-start(f32[2,256]{1,0:T(2,128)S(1)} %get-tuple-element.100), channel_id=1, source_target_pairs={{0,16},{16,32},{32,48},{48,64},{64,80},{80,96},{96,112},{112,128},... | collective-permute-start | bytes 6152 | tf_op jit(solution)/shard_map/ppermute | solution.py:47
  50.1 1.3 collective-permute-start.9
  51.4 9.4 %collective-permute-start.6 = (f32[260,2]{1,0:T(8,128)}, f32[260,2]{1,0:T(8,128)}, u32[]{:S(2)}, u32[]{:S(2)}) collective-permute-start(f32[260,2]{1,0:T(8,128)} %get-tuple-element.98), channel_id=1, source_target_pairs={{0,1},{1,2},{2,3},{3,4},{4,5},{5,6},{6,7},{7,8},{8,9},{9,10},{10,1... | collective-permute-start | bytes 6248 | tf_op jit(solution)/shard_map/ppermute | solution.py:47
  61.0 1.9 %collective-permute-start.7 = (f32[260,2]{1,0:T(8,128)}, f32[260,2]{1,0:T(8,128)}, u32[]{:S(2)}, u32[]{:S(2)}) collective-permute-start(f32[260,2]{1,0:T(8,128)} %get-tuple-element.99), channel_id=1, source_target_pairs={{1,0},{2,1},{3,2},{4,3},{5,4},{6,5},{7,6},{8,7},{9,8},{10,9},{11,1... | collective-permute-start | bytes 6248 | tf_op jit(solution)/shard_map/ppermute | solution.py:49
  62.9 7.5 %collective-permute-start.2 = (f32[260,2]{1,0:T(8,128)S(1)}, f32[260,2]{1,0:T(8,128)S(1)}, u32[]{:S(2)}, u32[]{:S(2)}) collective-permute-start(f32[260,2]{1,0:T(8,128)S(1)} %get-tuple-element.94), channel_id=1, source_target_pairs={{0,1},{1,2},{2,3},{3,4},{4,5},{5,6},{6,7},{7,8},{8,9},{9,10},{10,1... | collective-permute-start | bytes 6248 | tf_op jit(solution)/shard_map/ppermute | solution.py:47
  70.7 1.9 %collective-permute-start.3 = (f32[260,2]{1,0:T(8,128)S(1)}, f32[260,2]{1,0:T(8,128)S(1)}, u32[]{:S(2)}, u32[]{:S(2)}) collective-permute-start(f32[260,2]{1,0:T(8,128)S(1)} %get-tuple-element.95), channel_id=1, source_target_pairs={{1,0},{2,1},{3,2},{4,3},{5,4},{6,5},{7,6},{8,7},{9,8},{10,9},{11,1... | collective-permute-start | bytes 6248 | tf_op jit(solution)/shard_map/ppermute | solution.py:49
  72.6 7.5 %collective-permute-start.14 = (f32[260,2]{1,0:T(8,128)S(1)}, f32[260,2]{1,0:T(8,128)S(1)}, u32[]{:S(2)}, u32[]{:S(2)}) collective-permute-start(f32[260,2]{1,0:T(8,128)S(1)} %get-tuple-element.92), channel_id=1, source_target_pairs={{0,1},{1,2},{2,3},{3,4},{4,5},{5,6},{6,7},{7,8},{8,9},{9,10},{10,1... | collective-permute-start | bytes 6248 | tf_op jit(solution)/shard_map/ppermute | solution.py:47
  80.2 0.8 fusion.119
  80.9 1.9 %collective-permute-start.15 = (f32[260,2]{1,0:T(8,128)S(1)}, f32[260,2]{1,0:T(8,128)S(1)}, u32[]{:S(2)}, u32[]{:S(2)}) collective-permute-start(f32[260,2]{1,0:T(8,128)S(1)} %get-tuple-element.93), channel_id=1, source_target_pairs={{1,0},{2,1},{3,2},{4,3},{5,4},{6,5},{7,6},{8,7},{9,8},{10,9},{11,1... | collective-permute-start | bytes 6248 | tf_op jit(solution)/shard_map/ppermute | solution.py:49
  82.9 7.5 %collective-permute-start.18 = (f32[260,2]{1,0:T(8,128)S(1)}, f32[260,2]{1,0:T(8,128)S(1)}, u32[]{:S(2)}, u32[]{:S(2)}) collective-permute-start(f32[260,2]{1,0:T(8,128)S(1)} %get-tuple-element.96), channel_id=1, source_target_pairs={{0,1},{1,2},{2,3},{3,4},{4,5},{5,6},{6,7},{7,8},{8,9},{9,10},{10,1... | collective-permute-start | bytes 6248 | tf_op jit(solution)/shard_map/ppermute | solution.py:47
  90.7 1.9 %collective-permute-start.19 = (f32[260,2]{1,0:T(8,128)S(1)}, f32[260,2]{1,0:T(8,128)S(1)}, u32[]{:S(2)}, u32[]{:S(2)}) collective-permute-start(f32[260,2]{1,0:T(8,128)S(1)} %get-tuple-element.97), channel_id=1, source_target_pairs={{1,0},{2,1},{3,2},{4,3},{5,4},{6,5},{7,6},{8,7},{9,8},{10,9},{11,1... | collective-permute-start | bytes 6248 | tf_op jit(solution)/shard_map/ppermute | solution.py:49
  92.6 7.6 %collective-permute-start.10 = (f32[260,2]{1,0:T(8,128)}, f32[260,2]{1,0:T(8,128)}, u32[]{:S(2)}, u32[]{:S(2)}) collective-permute-start(f32[260,2]{1,0:T(8,128)} %get-tuple-element.90), channel_id=1, source_target_pairs={{0,1},{1,2},{2,3},{3,4},{4,5},{5,6},{6,7},{7,8},{8,9},{9,10},{10,1... | collective-permute-start | bytes 6248 | tf_op jit(solution)/shard_map/ppermute | solution.py:47
  100.4 1.9 %collective-permute-start.11 = (f32[260,2]{1,0:T(8,128)}, f32[260,2]{1,0:T(8,128)}, u32[]{:S(2)}, u32[]{:S(2)}) collective-permute-start(f32[260,2]{1,0:T(8,128)} %get-tuple-element.91), channel_id=1, source_target_pairs={{1,0},{2,1},{3,2},{4,3},{5,4},{6,5},{7,6},{8,7},{9,8},{10,9},{11,1... | collective-permute-start | bytes 6248 | tf_op jit(solution)/shard_map/ppermute | solution.py:49
  102.8 0.8 collective-permute-done.10
  103.6 8.2 %collective-permute-done.11 = f32[260,2]{1,0:T(8,128)} collective-permute-done((f32[260,2]{1,0:T(8,128)}, f32[260,2]{1,0:T(8,128)}, u32[]{:S(2)}, u32[]{:S(2)}) %collective-permute-start.11) | collective-permute-done | bytes 2112 | tf_op jit(solution)/shard_map/ppermute | solution.py:49
  111.7 1.2 pad_maximum_fusion.2
  112.9 1.2 fusion.29
  114.7 1.1 fusion.16
  115.8 14.5 %all-to-all-start.1 = ((f32[16,8,256]{2,1,0:T(8,128)}), f32[16,8,256]{2,1,0:T(8,128)S(1)}, u32[]{:S(2)}, u32[]{:S(2)}) async-start(f32[16,8,256]{2,1,0:T(8,128)} %fusion.16), calls=%async_computation.1 | async-start | bytes 262144 | tf_op jit(solution)/shard_map/all_to_all | solution.py:19
  130.4 1.4 fusion.35
  132.0 6.1 %all-to-all-done.1 = f32[16,8,256]{2,1,0:T(8,128)S(1)} async-done(((f32[16,8,256]{2,1,0:T(8,128)}), f32[16,8,256]{2,1,0:T(8,128)S(1)}, u32[]{:S(2)}, u32[]{:S(2)}) %all-to-all-start.1) | async-done | bytes 131104 | tf_op jit(solution)/shard_map/all_to_all | solution.py:19
  138.8 9.5 %all-to-all-start.2 = ((f32[16,2,256]{2,1,0:T(2,128)}), f32[16,2,256]{2,1,0:T(2,128)S(1)}, u32[]{:S(2)}, u32[]{:S(2)}) async-start(f32[16,2,256]{2,1,0:T(2,128)} %broadcast_in_dim.20), calls=%async_computation.2 | async-start | bytes 65536 | tf_op jit(solution)/shard_map/all_to_all | solution.py:25
  148.3 1.2 pad_maximum_fusion.1
  149.5 8.5 %all-to-all-done.2 = f32[16,2,256]{2,1,0:T(2,128)S(1)} async-done(((f32[16,2,256]{2,1,0:T(2,128)}), f32[16,2,256]{2,1,0:T(2,128)S(1)}, u32[]{:S(2)}, u32[]{:S(2)}) %all-to-all-start.2) | async-done | bytes 32800 | tf_op jit(solution)/shard_map/all_to_all | solution.py:25
  158.0 2.8 %fusion = f32[2,260]{1,0:T(2,128)S(1)} fusion(f32[2,4096]{1,0:T(2,128)S(1)} %bitcast.48, s32[4096]{0:T(1024)} %param.24, s32[260]{0:T(512)S(1)} %iota_add_fusion), kind=kOutput, calls=%fused_computation | convolution fusion | flops 26624000 | bytes 52272 | tf_op jit(solution)/shard_map/dot_general | solution.py:134
  161.0 1.2 fusion.27
  162.2 0.7 fusion.39
  163.0 0.9 fusion.33
  164.0 0.7 copy-done.2
  164.6 1.3 scatter.26
  166.0 1.6 fusion.58
  167.6 2.8 %fusion.51 = (f32[256,257]{1,0:T(8,128)S(1)}, f32[256,257]{1,0:T(8,128)}) fusion(f32[260,260]{1,0:T(8,128)S(1)} %scatter.24, f32[258,258]{1,0:T(8,128)S(1)} %scatter.25, f32[258,258]{1,0:T(8,128)} %scatter.26, f32[260,260]{1,0:T(8,128)S(1)} %scatter.20, f32[258,258]{1,0:T(8,128)S(1)} %slice_sqrt_fusion), kind=kLoop, calls=%fused_computation.81 | loop fusion | flops 1118464 | bytes 3158016 | tf_op jit(solution)/shard_map/mul | solution.py:72
  170.9 0.8 fusion.56
  171.8 1.5 fusion.63
  (89 shorter events, 6.3 us)
Async XLA Ops:
  0.6 0.7 copy-start
  1.9 6.4 %copy-start.1 = (bf16[2,16,32,4096]{3,2,1,0:T(8,128)(2,1)S(1)}, bf16[2,16,32,4096]{3,2,1,0:T(8,128)(2,1)}, u32[]{:S(2)}) copy-start(bf16[2,16,32,4096]{3,2,1,0:T(8,128)(2,1)} %param.20) | copy-start | bytes 25165828
  8.9 15.3 %copy-start.10 = (f32[256,256]{1,0:T(8,128)S(1)}, f32[256,256]{1,0:T(8,128)}, u32[]{:S(2)}) copy-start(f32[256,256]{1,0:T(8,128)} %param.25) | copy-start | bytes 786436
  8.9 19.7 %copy-start.11 = (s32[256,256]{1,0:T(8,128)S(1)}, s32[256,256]{1,0:T(8,128)}, u32[]{:S(2)}) copy-start(s32[256,256]{1,0:T(8,128)} %param.23) | copy-start | bytes 786436
  8.9 25.0 %copy-start.7 = (f32[256,256]{1,0:T(8,128)S(1)}, f32[256,256]{1,0:T(8,128)}, u32[]{:S(2)}) copy-start(f32[256,256]{1,0:T(8,128)} %param.22) | copy-start | bytes 786436
  8.9 29.0 %copy-start.8 = (f32[256,256]{1,0:T(8,128)S(1)}, f32[256,256]{1,0:T(8,128)}, u32[]{:S(2)}) copy-start(f32[256,256]{1,0:T(8,128)} %param.27) | copy-start | bytes 786436
  9.0 29.0 %copy-start.9 = (f32[256,256]{1,0:T(8,128)S(1)}, f32[256,256]{1,0:T(8,128)}, u32[]{:S(2)}) copy-start(f32[256,256]{1,0:T(8,128)} %param.26) | copy-start | bytes 786436
  11.6 102.6 %all-to-all-start = ((f32[16,2,16,256]{3,2,1,0:T(8,128)}), f32[16,2,16,256]{3,2,1,0:T(8,128)S(1)}, u32[]{:S(2)}, u32[]{:S(2)}) async-start(f32[16,2,16,256]{3,2,1,0:T(8,128)} %copy.13), calls=%async_computation | async-start | bytes 1048576 | tf_op jit(solution)/shard_map/all_to_all | solution.py:19
  24.2 13.9 %collective-permute-start.4 = (f32[2,256]{1,0:T(2,128)S(1)}, f32[2,256]{1,0:T(2,128)S(1)}, u32[]{:S(2)}, u32[]{:S(2)}) collective-permute-start(f32[2,256]{1,0:T(2,128)S(1)} %get-tuple-element.108), channel_id=1, source_target_pairs={{0,16},{16,32},{32,48},{48,64},{64,80},{80,96},{96,112},{112,128},... | collective-permute-start | bytes 6152 | tf_op jit(solution)/shard_map/ppermute | solution.py:47
  27.3 12.0 %collective-permute-start.5 = (f32[2,256]{1,0:T(2,128)S(1)}, f32[2,256]{1,0:T(2,128)S(1)}, u32[]{:S(2)}, u32[]{:S(2)}) collective-permute-start(f32[2,256]{1,0:T(2,128)S(1)} %get-tuple-element.109), channel_id=1, source_target_pairs={{16,0},{32,16},{48,32},{64,48},{80,64},{96,80},{112,96},{128,112},... | collective-permute-start | bytes 6152 | tf_op jit(solution)/shard_map/ppermute | solution.py:49
  28.6 15.5 %collective-permute-start = (f32[2,256]{1,0:T(2,128)S(1)}, f32[2,256]{1,0:T(2,128)S(1)}, u32[]{:S(2)}, u32[]{:S(2)}) collective-permute-start(f32[2,256]{1,0:T(2,128)S(1)} %get-tuple-element.104), channel_id=1, source_target_pairs={{0,16},{16,32},{32,48},{48,64},{64,80},{80,96},{96,112},{112,128},... | collective-permute-start | bytes 6152 | tf_op jit(solution)/shard_map/ppermute | solution.py:47
  32.6 12.8 %collective-permute-start.1 = (f32[2,256]{1,0:T(2,128)S(1)}, f32[2,256]{1,0:T(2,128)S(1)}, u32[]{:S(2)}, u32[]{:S(2)}) collective-permute-start(f32[2,256]{1,0:T(2,128)S(1)} %get-tuple-element.105), channel_id=1, source_target_pairs={{16,0},{32,16},{48,32},{64,48},{80,64},{96,80},{112,96},{128,112},... | collective-permute-start | bytes 6152 | tf_op jit(solution)/shard_map/ppermute | solution.py:49
  34.0 16.2 %collective-permute-start.12 = (f32[2,256]{1,0:T(2,128)S(1)}, f32[2,256]{1,0:T(2,128)S(1)}, u32[]{:S(2)}, u32[]{:S(2)}) collective-permute-start(f32[2,256]{1,0:T(2,128)S(1)} %get-tuple-element.102), channel_id=1, source_target_pairs={{0,16},{16,32},{32,48},{48,64},{64,80},{80,96},{96,112},{112,128},... | collective-permute-start | bytes 6152 | tf_op jit(solution)/shard_map/ppermute | solution.py:47
  38.0 13.4 %collective-permute-start.13 = (f32[2,256]{1,0:T(2,128)S(1)}, f32[2,256]{1,0:T(2,128)S(1)}, u32[]{:S(2)}, u32[]{:S(2)}) collective-permute-start(f32[2,256]{1,0:T(2,128)S(1)} %get-tuple-element.103), channel_id=1, source_target_pairs={{16,0},{32,16},{48,32},{64,48},{80,64},{96,80},{112,96},{128,112},... | collective-permute-start | bytes 6152 | tf_op jit(solution)/shard_map/ppermute | solution.py:49
  39.3 21.7 %collective-permute-start.16 = (f32[2,256]{1,0:T(2,128)S(1)}, f32[2,256]{1,0:T(2,128)S(1)}, u32[]{:S(2)}, u32[]{:S(2)}) collective-permute-start(f32[2,256]{1,0:T(2,128)S(1)} %get-tuple-element.106), channel_id=1, source_target_pairs={{0,16},{16,32},{32,48},{48,64},{64,80},{80,96},{96,112},{112,128},... | collective-permute-start | bytes 6152 | tf_op jit(solution)/shard_map/ppermute | solution.py:47
  44.1 18.8 %collective-permute-start.17 = (f32[2,256]{1,0:T(2,128)S(1)}, f32[2,256]{1,0:T(2,128)S(1)}, u32[]{:S(2)}, u32[]{:S(2)}) collective-permute-start(f32[2,256]{1,0:T(2,128)S(1)} %get-tuple-element.107), channel_id=1, source_target_pairs={{16,0},{32,16},{48,32},{64,48},{80,64},{96,80},{112,96},{128,112},... | collective-permute-start | bytes 6152 | tf_op jit(solution)/shard_map/ppermute | solution.py:49
  45.4 25.2 %collective-permute-start.8 = (f32[2,256]{1,0:T(2,128)S(1)}, f32[2,256]{1,0:T(2,128)S(1)}, u32[]{:S(2)}, u32[]{:S(2)}) collective-permute-start(f32[2,256]{1,0:T(2,128)S(1)} %get-tuple-element.100), channel_id=1, source_target_pairs={{0,16},{16,32},{32,48},{48,64},{64,80},{80,96},{96,112},{112,128},... | collective-permute-start | bytes 6152 | tf_op jit(solution)/shard_map/ppermute | solution.py:47
  50.1 22.5 %collective-permute-start.9 = (f32[2,256]{1,0:T(2,128)S(1)}, f32[2,256]{1,0:T(2,128)S(1)}, u32[]{:S(2)}, u32[]{:S(2)}) collective-permute-start(f32[2,256]{1,0:T(2,128)S(1)} %get-tuple-element.101), channel_id=1, source_target_pairs={{16,0},{32,16},{48,32},{64,48},{80,64},{96,80},{112,96},{128,112},... | collective-permute-start | bytes 6152 | tf_op jit(solution)/shard_map/ppermute | solution.py:49
  51.4 96.8 %collective-permute-start.6 = (f32[260,2]{1,0:T(8,128)}, f32[260,2]{1,0:T(8,128)}, u32[]{:S(2)}, u32[]{:S(2)}) collective-permute-start(f32[260,2]{1,0:T(8,128)} %get-tuple-element.98), channel_id=1, source_target_pairs={{0,1},{1,2},{2,3},{3,4},{4,5},{5,6},{6,7},{7,8},{8,9},{9,10},{10,1... | collective-permute-start | bytes 6248 | tf_op jit(solution)/shard_map/ppermute | solution.py:47
  61.0 87.3 %collective-permute-start.7 = (f32[260,2]{1,0:T(8,128)}, f32[260,2]{1,0:T(8,128)}, u32[]{:S(2)}, u32[]{:S(2)}) collective-permute-start(f32[260,2]{1,0:T(8,128)} %get-tuple-element.99), channel_id=1, source_target_pairs={{1,0},{2,1},{3,2},{4,3},{5,4},{6,5},{7,6},{8,7},{9,8},{10,9},{11,1... | collective-permute-start | bytes 6248 | tf_op jit(solution)/shard_map/ppermute | solution.py:49
  62.9 18.0 %collective-permute-start.2 = (f32[260,2]{1,0:T(8,128)S(1)}, f32[260,2]{1,0:T(8,128)S(1)}, u32[]{:S(2)}, u32[]{:S(2)}) collective-permute-start(f32[260,2]{1,0:T(8,128)S(1)} %get-tuple-element.94), channel_id=1, source_target_pairs={{0,1},{1,2},{2,3},{3,4},{4,5},{5,6},{6,7},{7,8},{8,9},{9,10},{10,1... | collective-permute-start | bytes 6248 | tf_op jit(solution)/shard_map/ppermute | solution.py:47
  70.7 12.2 %collective-permute-start.3 = (f32[260,2]{1,0:T(8,128)S(1)}, f32[260,2]{1,0:T(8,128)S(1)}, u32[]{:S(2)}, u32[]{:S(2)}) collective-permute-start(f32[260,2]{1,0:T(8,128)S(1)} %get-tuple-element.95), channel_id=1, source_target_pairs={{1,0},{2,1},{3,2},{4,3},{5,4},{6,5},{7,6},{8,7},{9,8},{10,9},{11,1... | collective-permute-start | bytes 6248 | tf_op jit(solution)/shard_map/ppermute | solution.py:49
  72.6 18.1 %collective-permute-start.14 = (f32[260,2]{1,0:T(8,128)S(1)}, f32[260,2]{1,0:T(8,128)S(1)}, u32[]{:S(2)}, u32[]{:S(2)}) collective-permute-start(f32[260,2]{1,0:T(8,128)S(1)} %get-tuple-element.92), channel_id=1, source_target_pairs={{0,1},{1,2},{2,3},{3,4},{4,5},{5,6},{6,7},{7,8},{8,9},{9,10},{10,1... | collective-permute-start | bytes 6248 | tf_op jit(solution)/shard_map/ppermute | solution.py:47
  80.9 11.6 %collective-permute-start.15 = (f32[260,2]{1,0:T(8,128)S(1)}, f32[260,2]{1,0:T(8,128)S(1)}, u32[]{:S(2)}, u32[]{:S(2)}) collective-permute-start(f32[260,2]{1,0:T(8,128)S(1)} %get-tuple-element.93), channel_id=1, source_target_pairs={{1,0},{2,1},{3,2},{4,3},{5,4},{6,5},{7,6},{8,7},{9,8},{10,9},{11,1... | collective-permute-start | bytes 6248 | tf_op jit(solution)/shard_map/ppermute | solution.py:49
  82.9 17.5 %collective-permute-start.18 = (f32[260,2]{1,0:T(8,128)S(1)}, f32[260,2]{1,0:T(8,128)S(1)}, u32[]{:S(2)}, u32[]{:S(2)}) collective-permute-start(f32[260,2]{1,0:T(8,128)S(1)} %get-tuple-element.96), channel_id=1, source_target_pairs={{0,1},{1,2},{2,3},{3,4},{4,5},{5,6},{6,7},{7,8},{8,9},{9,10},{10,1... | collective-permute-start | bytes 6248 | tf_op jit(solution)/shard_map/ppermute | solution.py:47
  90.7 11.7 %collective-permute-start.19 = (f32[260,2]{1,0:T(8,128)S(1)}, f32[260,2]{1,0:T(8,128)S(1)}, u32[]{:S(2)}, u32[]{:S(2)}) collective-permute-start(f32[260,2]{1,0:T(8,128)S(1)} %get-tuple-element.97), channel_id=1, source_target_pairs={{1,0},{2,1},{3,2},{4,3},{5,4},{6,5},{7,6},{8,7},{9,8},{10,9},{11,1... | collective-permute-start | bytes 6248 | tf_op jit(solution)/shard_map/ppermute | solution.py:49
  92.6 11.0 %collective-permute-start.10 = (f32[260,2]{1,0:T(8,128)}, f32[260,2]{1,0:T(8,128)}, u32[]{:S(2)}, u32[]{:S(2)}) collective-permute-start(f32[260,2]{1,0:T(8,128)} %get-tuple-element.90), channel_id=1, source_target_pairs={{0,1},{1,2},{2,3},{3,4},{4,5},{5,6},{6,7},{7,8},{8,9},{9,10},{10,1... | collective-permute-start | bytes 6248 | tf_op jit(solution)/shard_map/ppermute | solution.py:47
  100.4 11.3 %collective-permute-start.11 = (f32[260,2]{1,0:T(8,128)}, f32[260,2]{1,0:T(8,128)}, u32[]{:S(2)}, u32[]{:S(2)}) collective-permute-start(f32[260,2]{1,0:T(8,128)} %get-tuple-element.91), channel_id=1, source_target_pairs={{1,0},{2,1},{3,2},{4,3},{5,4},{6,5},{7,6},{8,7},{9,8},{10,9},{11,1... | collective-permute-start | bytes 6248 | tf_op jit(solution)/shard_map/ppermute | solution.py:49
  115.8 22.3 %all-to-all-start.1 = ((f32[16,8,256]{2,1,0:T(8,128)}), f32[16,8,256]{2,1,0:T(8,128)S(1)}, u32[]{:S(2)}, u32[]{:S(2)}) async-start(f32[16,8,256]{2,1,0:T(8,128)} %fusion.16), calls=%async_computation.1 | async-start | bytes 262144 | tf_op jit(solution)/shard_map/all_to_all | solution.py:19
  138.2 24.8 %copy-start.12 = (f32[8,256]{1,0:T(8,128)}, f32[8,256]{1,0:T(8,128)S(1)}, u32[]{:S(2)}) copy-start(f32[8,256]{1,0:T(8,128)S(1)} %reduce_sum.19) | copy-start | bytes 24580
  138.8 19.2 %all-to-all-start.2 = ((f32[16,2,256]{2,1,0:T(2,128)}), f32[16,2,256]{2,1,0:T(2,128)S(1)}, u32[]{:S(2)}, u32[]{:S(2)}) async-start(f32[16,2,256]{2,1,0:T(2,128)} %broadcast_in_dim.20), calls=%async_computation.2 | async-start | bytes 65536 | tf_op jit(solution)/shard_map/all_to_all | solution.py:25
  161.0 1.9 %copy-start.4 = (f32[258,259]{1,0:T(8,128)S(1)}, f32[258,259]{1,0:T(8,128)}, u32[]{:S(2)}) copy-start(f32[258,259]{1,0:T(8,128)} %fusion.29) | copy-start | bytes 801868
  161.0 1.9 %copy-start.5 = (f32[259,258]{1,0:T(8,128)S(1)}, f32[259,258]{1,0:T(8,128)}, u32[]{:S(2)}) copy-start(f32[259,258]{1,0:T(8,128)} %fusion.35) | copy-start | bytes 801868
  163.9 0.7 copy-start.2
  167.6 4.1 %copy-start.3 = (f32[258,258]{1,0:T(8,128)S(1)}, f32[258,258]{1,0:T(8,128)}, u32[]{:S(2)}) copy-start(f32[258,258]{1,0:T(8,128)} %scatter.26) | copy-start | bytes 798772
  170.4 1.4 copy-start.6
where the time goes:
time: 174 us; the launch traced here: 173 us
  starting transfers between devices  112 us (64%)
  waiting for transfers between devices  23.6 us (14%)
  other arithmetic  16.6 us (10%)
  matrix products  12.6 us (7%)
  local copies, waits for them, and re-layouts  7.15 us (4%)
    ppermute x10, starting transfers between devices, with_halo(): lax.ppermute(tail, axis, [(i, (i + 1) % count) for i in range(ends)])  59.2 us
    all_to_all x2, starting transfers between devices, summed_on_arrival(): tiles = lax.all_to_all(split_up(x, dim, length), axis, 0, 0, tiled=True)  27.1 us
    ppermute x10, starting transfers between devices, with_halo(): lax.ppermute(head, axis, [((i + 1) % count, i) for i in range(ends)])  16 us
    all_to_all x1, starting transfers between devices, copy_for_each(): return lax.all_to_all(copies, axis, split_axis=0, concat_axis=0, tiled=True)  9.47 us
    all_to_all x1, waiting for transfers between devices, copy_for_each(): return lax.all_to_all(copies, axis, split_axis=0, concat_axis=0, tiled=True)  8.5 us
    ppermute x10, waiting for transfers between devices, with_halo(): lax.ppermute(head, axis, [((i + 1) % count, i) for i in range(ends)])  8.2 us
    all_to_all x2, waiting for transfers between devices, summed_on_arrival(): tiles = lax.all_to_all(split_up(x, dim, length), axis, 0, 0, tiled=True)  6.14 us
    mul x4, other arithmetic, face_fluxes(): opened * (0.5 * (left_sq * left_surf + right_sq * right_surf) - damping *...  5.47 us
  transfers between devices with their start and end apart: 23, of which 4 were waited for; matrix products, arithmetic and copies ran while one was open for 6% of the time, Pallas kernels for 0%

commit v1 on v0

v1 whole, which is shorter than its diff:
```python
import functools

import jax
import jax.numpy as jnp
import numpy as np
from jax import lax
from jax.experimental import pallas as pl
from jax.experimental.pallas import tpu as pltpu
from jax.sharding import PartitionSpec as P

F32 = jnp.float32
BF16 = jnp.bfloat16
HIGH = lax.Precision.HIGHEST
MESH = pl.DeviceIdType.MESH
ORDER = (2, 1, 3, 0)


def transform_tables():
    table = np.zeros((16, 128, 128), np.float32)
    times = np.arange(128)
    inner = times.reshape(4, 4, 8).transpose(1, 0, 2).reshape(-1)
    for row in range(16):
        freqs = row * 16 + np.arange(16)
        angle = 2.0 * np.pi * ((freqs[:, None] * inner[None, :]) % 256) / 256.0
        table[row, 0:16] = np.cos(angle) / 256.0
        table[row, 16:32] = -np.sin(angle) / 256.0
        angle = 2.0 * np.pi * ((freqs[:, None] * times[None, :]) % 256) / 256.0
        table[row, 32:48] = np.cos(angle)
        table[row, 48:64] = -np.sin(angle)
        table[row, 64:80] = np.sin(angle)
        table[row, 80:96] = np.cos(angle)
    return table


def after(values, axis):
    return pltpu.roll(values, values.shape[axis] - 1, axis)


def before(values, axis):
    return pltpu.roll(values, 1, axis)


def face_terms(speed, wet):
    celerity = jnp.sqrt(speed)
    terms = []
    for axis in (1, 0):
        opened = wet * after(wet, axis)
        terms.append((0.5 * opened, opened * (0.25 * (celerity + after(celerity, axis)))))
    return terms


def advance(surface, along_x, along_y, speed, wet, terms):
    pressure = speed * surface
    changes = []
    for axis, along, across in ((1, along_x, along_y), (0, along_y, along_x)):
        half, damp = terms[1 - axis]
        next_along = after(along, axis)
        mass = half * (along + next_along) - damp * (after(surface, axis) - surface)
        push = half * (pressure + after(pressure, axis)) - damp * (next_along - along)
        shear = damp * (across - after(across, axis))
        changes.append(tuple(flux - before(flux, axis) for flux in (mass, push, shear)))
    (mass_x, push_x, shear_x), (mass_y, push_y, shear_y) = changes
    return (
        wet * (surface - 0.25 * (mass_x + mass_y)),
        wet * (along_x - 0.25 * (push_x + shear_y)),
        wet * (along_y - 0.25 * (shear_x + push_y)),
    )


def kernel(
    kern, coef, speed, mask, cells, surf, flow_x, flow_y, table,
    series_o, surf_o, flow_x_o, flow_y_o,
    kbuf, tab, cbuf, mbuf, cellbuf, left, own, dsend, drecv, ysend, yrecv,
    xsend, xrecv, zsend, zrecv, gsend, grecv, fields, ewsend, ewrecv, onehot, latest,
    ksem, lsem, dsem, ysem, xsem, zsem, gssem, grsem, nssem, ewsem,
):
    row, col = lax.axis_index("rows"), lax.axis_index("cols")
    x, z_lo = row % 4, row // 4
    y, z_hi, core = col // 4, (col // 2) % 2, col % 2
    z = z_hi * 4 + z_lo
    is_edge = row == 15

    def place(at_x, at_y, at_z, at_core):
        return ((at_z % 4) * 4 + at_x, at_y * 4 + (at_z // 4) * 2 + at_core)

    partner = place(x, y, z, 1 - core)
    y_peer = [place(x, (y + d) % 4, z, core) for d in range(4)]
    x_peer = [place((x + d) % 4, y, z, core) for d in range(4)]
    z_peer = [place(x, y, (z + d) % 8, core) for d in range(8)]
    north, south = ((row + 15) % 16, col), ((row + 1) % 16, col)
    west, east = (row, (col + 15) % 16), (row, (col + 1) % 16)

    barrier = pltpu.get_barrier_semaphore()
    for peer in [partner, *y_peer[1:], *x_peer[1:], *z_peer[1:], north, south, west, east]:
        pl.semaphore_signal(barrier, inc=1, device_id=peer, device_id_type=MESH)

    @pl.when(is_edge)
    def _():
        def greet(index, carry):
            at_z, at_col = index // 8, index % 8
            peer = place(3, at_col // 2, at_z, at_col % 2)

            @pl.when((peer[0] != row) | (peer[1] != col))
            def _():
                pl.semaphore_signal(barrier, inc=1, device_id=peer, device_id_type=MESH)

            return carry

        lax.fori_loop(0, 64, greet, 0)

    local = [
        pltpu.make_async_copy(table.at[row], tab, lsem.at[0]),
        pltpu.make_async_copy(coef, cbuf, lsem.at[1]),
    ]
    for copy in local:
        copy.start()
    loads = []
    for i, d in enumerate(ORDER):
        for side, par in enumerate((1 - core, core)):
            for part in range(2):
                slot = i * 4 + side * 2 + part
                start = pl.multiple_of(((((y + d) % 4) * 2 + part) * 2 + par) * 256, 256)
                copy = pltpu.make_async_copy(
                    kern.at[:, pl.ds(start, 256)], kbuf.at[slot], ksem.at[slot]
                )
                copy.start()
                loads.append(copy)
    inner = (pl.ds(8, 256), pl.ds(0, 256))
    grids = [
        pltpu.make_async_copy(ref, fields.at[(j, *inner)], lsem.at[2 + j])
        for j, ref in enumerate((surf, flow_x, flow_y, speed))
    ]
    grids += [
        pltpu.make_async_copy(mask, mbuf, lsem.at[6]),
        pltpu.make_async_copy(cells, cellbuf, lsem.at[7]),
    ]
    for copy in grids:
        copy.start()

    for copy in local:
        copy.wait()
    tables = tab[...]
    coefs = jnp.dot(tables[32:96], cbuf[...], precision=HIGH, preferred_element_type=F32)
    lanes = lax.broadcasted_iota(jnp.int32, (32, 512), 1)
    subs = lax.broadcasted_iota(jnp.int32, (32, 512), 0)
    spread = (lanes % 32 == subs).astype(F32).astype(BF16)
    tiled = jnp.dot(coefs.astype(BF16), spread, preferred_element_type=F32)
    diagonal = lanes // 32 == subs % 16
    left[:, 0:512] = jnp.where(diagonal, tiled[0:32], 0.0).astype(BF16)
    left[:, 512:1024] = jnp.where(diagonal, tiled[32:64], 0.0).astype(BF16)

    dcopy, ycopy = [], {}

    def merge(i):
        d = ORDER[i]
        dcopy[i].wait_recv()
        total = own[i] + drecv[i]
        if d == 0:
            own[i] = total
            return
        ysend[d - 1] = total
        ycopy[d] = pltpu.make_async_remote_copy(
            src_ref=ysend.at[d - 1], dst_ref=yrecv.at[d - 1],
            send_sem=ysem.at[0, d - 1], recv_sem=ysem.at[1, d - 1],
            device_id=y_peer[d], device_id_type=MESH,
        )
        ycopy[d].start()

    for i in range(4):
        for side in range(2):
            for part in range(2):
                slot = i * 4 + side * 2 + part
                loads[slot].wait()
                spec = jnp.dot(left[...], kbuf[slot], preferred_element_type=F32)
                target = own if side else dsend
                target[i, :, part * 256 : part * 256 + 256] = spec
            if side == 0:
                if i == 0:
                    pl.semaphore_wait(
                        barrier, 18 + jnp.where(x == 3, 16 - is_edge.astype(jnp.int32), 0)
                    )
                copy = pltpu.make_async_remote_copy(
                    src_ref=dsend.at[i], dst_ref=drecv.at[i],
                    send_sem=dsem.at[0, i], recv_sem=dsem.at[1, i],
                    device_id=partner, device_id_type=MESH,
                )
                copy.start()
                dcopy.append(copy)
        if i >= 1:
            merge(i - 1)

    for copy in grids:
        copy.wait()
    fields[(4, *inner)] = mbuf[...].astype(F32)
    ns_copies = []
    for at, (first, last, peer) in enumerate(((8, 264, north), (256, 0, south))):
        copy = pltpu.make_async_remote_copy(
            src_ref=fields.at[:, pl.ds(first, 8), pl.ds(0, 256)],
            dst_ref=fields.at[:, pl.ds(last, 8), pl.ds(0, 256)],
            send_sem=nssem.at[0, at], recv_sem=nssem.at[1, at],
            device_id=peer, device_id_type=MESH,
        )
        copy.start()
        ns_copies.append(copy)
    merge(3)

    def select(block, carry):
        at = lax.broadcasted_iota(jnp.int32, (384, 128), 0)
        column = col * 256 + jnp.where(at >= 320, at - 384, at)
        found = cellbuf[pl.ds(block, 1), :] == column
        onehot[:, pl.ds(pl.multiple_of(block * 128, 128), 128)] = jnp.where(
            found, 1.0, 0.0
        ).astype(BF16)
        return carry

    @pl.when(is_edge)
    def _():
        lax.fori_loop(0, 32, select, 0)

    for copy in ns_copies:
        copy.wait_recv()

    @pl.when(row == 0)
    def _():
        fields[:, 0:8, 0:256] = jnp.zeros((5, 8, 256), F32)

    @pl.when(is_edge)
    def _():
        fields[:, 264:272, 0:256] = jnp.zeros((5, 8, 256), F32)

    lane = lax.broadcasted_iota(jnp.int32, (272, 128), 1)
    ew_copies = []
    for at, (first, shift, peer) in enumerate(((0, 0, west), (128, 2, east))):
        packed = jnp.zeros((272, 128), F32)
        for j in range(5):
            block = fields[j, :, first : first + 128]
            if 2 * j + shift:
                block = pltpu.roll(block, 2 * j + shift, 1)
            packed = jnp.where(lane // 2 == j, block, packed)
        packed = jnp.concatenate([packed, jnp.zeros((112, 128), F32)], axis=0)
        ewsend[at] = packed.T[0:16]
        copy = pltpu.make_async_remote_copy(
            src_ref=ewsend.at[at], dst_ref=ewrecv.at[at],
            send_sem=ewsem.at[0, at], recv_sem=ewsem.at[1, at],
            device_id=peer, device_id_type=MESH,
        )
        copy.start()
        ew_copies.append(copy)

    total = own[3]
    for d in (1, 3, 2):
        ycopy[d].wait_recv()
        total = total + yrecv[d - 1]
    inverse = tables.T[:, 0:32]
    partial = jnp.dot(inverse, total, precision=HIGH, preferred_element_type=F32)
    for at in range(4):
        xsend[at] = partial[at * 32 : at * 32 + 32]
    xcopy = {}
    for d in (2, 1, 3):
        xcopy[d] = pltpu.make_async_remote_copy(
            src_ref=xsend.at[(x + d) % 4], dst_ref=xrecv.at[d - 1],
            send_sem=xsem.at[0, d - 1], recv_sem=xsem.at[1, d - 1],
            device_id=x_peer[d], device_id_type=MESH,
        )
        xcopy[d].start()

    for copy in ew_copies:
        copy.wait_recv()
    sides = []
    for at, end in ((0, 15), (1, 0)):
        message = jnp.where(col == end, 0.0, ewrecv[at])
        padded = jnp.concatenate([message, jnp.zeros((112, 384), F32)], axis=0)
        sides.append(padded.T[0:272])
    for j in range(5):
        right = pltpu.roll(sides[0], 128 - 2 * j, 1) if j else sides[0]
        wrapped = pltpu.roll(sides[1], 126 - 2 * j, 1)
        fields[j, :, 256:384] = jnp.where(
            lane < 2, right, jnp.where(lane >= 126, wrapped, 0.0)
        )

    total = xsend[x]
    for d in (1, 3, 2):
        xcopy[d].wait_recv()
        total = total + xrecv[d - 1]
    zsend[0] = total[:, 0:256]
    zsend[1] = total[:, 256:512]
    gsend[...] = total[30:32]
    me = z * 8 + y * 2 + core

    def ghost_copy(index):
        return pltpu.make_async_remote_copy(
            src_ref=gsend, dst_ref=grecv.at[me],
            send_sem=gssem.at[index], recv_sem=grsem,
            device_id=(15, index), device_id_type=MESH,
        )

    @pl.when(x == 3)
    def _():
        def send(index, carry):
            @pl.when((row != 15) | (index != col))
            def _():
                ghost_copy(index).start()

            return carry

        lax.fori_loop(0, 16, send, 0)

    zcopy = {}
    for d in (4, 3, 5, 2, 6, 1, 7):
        to = (z + d) % 8
        zcopy[d] = pltpu.make_async_remote_copy(
            src_ref=zsend.at[to // 4, pl.ds(pl.multiple_of((to % 4) * 8, 8), 8)],
            dst_ref=zrecv.at[d - 1],
            send_sem=zsem.at[0, d - 1], recv_sem=zsem.at[1, d - 1],
            device_id=z_peer[d], device_id_type=MESH,
        )
        zcopy[d].start()

    def strip(at, carry):
        base = pl.multiple_of(at * 32, 8)
        state = [fields[j, pl.ds(base, 48), :] for j in range(5)]
        values, rest = state[0:3], state[3:5]
        terms = face_terms(*rest)
        for _ in range(2):
            values = advance(*values, *rest, terms)
        for ref, value in zip((surf_o, flow_x_o, flow_y_o), values):
            ref[pl.ds(base, 32), :] = value[8:40, 0:256]
        return carry

    lax.fori_loop(0, 8, strip, 0)

    total = zsend[z_hi, pl.ds(pl.multiple_of(z_lo * 8, 8), 8)]
    for d in range(1, 8):
        zcopy[d].wait_recv()
        total = total + zrecv[d - 1]
    series_o[...] = total

    @pl.when(is_edge)
    def _():
        grecv[me] = gsend[...]
        pltpu.make_async_copy(grecv.at[pl.ds(0, 63)], grecv.at[pl.ds(0, 63)], grsem).wait()
        latest[...] = jnp.zeros((8, 4096), F32)
        for at in range(8):
            summed = grecv[at]
            for other in range(1, 8):
                summed = summed + grecv[other * 8 + at]
            for part in range(2):
                first = ((at // 2 * 2 + part) * 2 + at % 2) * 256
                latest[0:2, first : first + 256] = summed[:, part * 256 : part * 256 + 256]
        value = latest[...]
        high = value.astype(BF16)
        value = value - high.astype(F32)
        middle = value.astype(BF16)
        low = (value - middle.astype(F32)).astype(BF16)
        ghost = jnp.zeros((8, 384), F32)
        for piece in (low, middle, high):
            ghost = ghost + lax.dot_general(
                piece, onehot[...], (((1,), (1,)), ((), ())), preferred_element_type=F32
            )
        beyond = lax.broadcasted_iota(jnp.int32, (24, 384), 0) == 16
        state = [fields[j, 248:272, :] for j in range(5)]
        rest = [jnp.where(beyond, 1.0, value) for value in state[3:5]]
        values = state[0:3]
        terms = face_terms(*rest)
        for step in range(2):
            values = [
                jnp.where(beyond, ghost[step : step + 1], values[0]),
                jnp.where(beyond, 0.0, values[1]),
                jnp.where(beyond, 0.0, values[2]),
            ]
            values = advance(*values, *rest, terms)
        for ref, value in zip((surf_o, flow_x_o, flow_y_o), values):
            ref[248:256, :] = value[8:16, 0:256]

    for copy in [*dcopy, *ycopy.values(), *xcopy.values(), *zcopy.values(), *ns_copies, *ew_copies]:
        copy.wait_send()

    @pl.when(x == 3)
    def _():
        def finish(index, carry):
            @pl.when((row != 15) | (index != col))
            def _():
                ghost_copy(index).wait_send()

            return carry

        lax.fori_loop(0, 16, finish, 0)


def on_device(
    kernel_hat, coefficients, wave_speed_sq, wet_mask, boundary_cell, height, flux_x, flux_y
):
    field = jax.ShapeDtypeStruct((256, 256), F32)
    dma = pltpu.SemaphoreType.DMA
    return pl.pallas_call(
        kernel,
        out_shape=(jax.ShapeDtypeStruct((8, 256), F32), field, field, field),
        in_specs=[pl.BlockSpec(memory_space=pltpu.MemorySpace.HBM)] * 9,
        out_specs=[pl.BlockSpec(memory_space=pltpu.VMEM)] * 4,
        scratch_shapes=[
            pltpu.VMEM((16, 1024, 256), BF16),
            pltpu.VMEM((128, 128), F32),
            pltpu.VMEM((128, 32), F32),
            pltpu.VMEM((256, 256), jnp.int32),
            pltpu.VMEM((32, 128), jnp.int32),
            pltpu.VMEM((32, 1024), BF16),
            pltpu.VMEM((4, 32, 512), F32),
            pltpu.VMEM((4, 32, 512), F32),
            pltpu.VMEM((4, 32, 512), F32),
            pltpu.VMEM((3, 32, 512), F32),
            pltpu.VMEM((3, 32, 512), F32),
            pltpu.VMEM((4, 32, 512), F32),
            pltpu.VMEM((3, 32, 512), F32),
            pltpu.VMEM((2, 32, 256), F32),
            pltpu.VMEM((7, 8, 256), F32),
            pltpu.VMEM((2, 512), F32),
            pltpu.VMEM((64, 2, 512), F32),
            pltpu.VMEM((5, 272, 384), F32),
            pltpu.VMEM((2, 16, 384), F32),
            pltpu.VMEM((2, 16, 384), F32),
            pltpu.VMEM((384, 4096), BF16),
            pltpu.VMEM((8, 4096), F32),
            dma((16,)),
            dma((8,)),
            dma((2, 4)),
            dma((2, 3)),
            dma((2, 3)),
            dma((2, 7)),
            dma((16,)),
            dma(()),
            dma((2, 2)),
            dma((2, 2)),
        ],
        compiler_params=pltpu.CompilerParams(
            collective_id=0, has_side_effects=True, vmem_limit_bytes=48 * 1024 * 1024
        ),
    )(
        kernel_hat.reshape(1024, 4096),
        coefficients,
        wave_speed_sq,
        wet_mask,
        boundary_cell.reshape(32, 128),
        height,
        flux_x,
        flux_y,
        jnp.asarray(transform_tables()),
    )


def solution(mesh):
    return jax.shard_map(
        on_device,
        mesh=mesh,
        in_specs=(
            P(None, "rows", "cols", None),
            P(None, "cols"),
            P("rows", "cols"),
            P("rows", "cols"),
            P(),
            P("rows", "cols"),
            P("rows", "cols"),
            P("rows", "cols"),
        ),
        out_specs=(P("rows", "cols"), P("rows", "cols"), P("rows", "cols"), P("rows", "cols")),
        check_vma=False,
    )
```

time: 174 us -> 43.4 us (0.25)
  starting transfers between devices: 112 us -> 0 us
  Pallas kernels: 0 us -> 32.1 us
  waiting for transfers between devices: 23.6 us -> 0 us
  other arithmetic: 16.6 us -> 0 us
  matrix products: 12.6 us -> 0 us
  local copies, waits for them, and re-layouts: 7.15 us -> 10.2 us
    ppermute x20 -> x0, starting transfers between devices: 75.3 us -> none  [the longest x10 59.2 us: with_halo(): lax.ppermute(tail, axis, [(i, (i + 1) % count) for i in range(ends)])]
    all_to_all x3 -> x0, starting transfers between devices: 36.6 us -> none  [the longest x2 27.1 us: summed_on_arrival(): tiles = lax.all_to_all(split_up(x, dim, length), axis, 0, 0, tiled=True)]
    pallas_call x0 -> x1, Pallas kernels: none -> 32.1 us  [on_device(): pl.pallas_call(kernel, out_shape=(jax.ShapeDtypeStruct((8, 256), F32), fi...]
    all_to_all x3 -> x0, waiting for transfers between devices: 14.6 us -> none  [the longest x1 8.5 us: copy_for_each(): return lax.all_to_all(copies, axis, split_axis=0, concat_axis=0, tiled=True)]
    mul x10 -> x0, other arithmetic: 12.7 us -> none  [the longest x4 5.47 us: face_fluxes(): opened * (0.5 * (left_sq * left_surf + right_sq * right_surf) - damping *...]
    dot_general x9 -> x0, matrix products: 12.6 us -> none  [the longest x1 3.35 us: on_device(): jnp.einsum(form, kern_im, coef_re, preferred_element_type=jnp.float32)]
    ppermute x20 -> x0, waiting for transfers between devices: 8.98 us -> none  [the longest x10 8.2 us: with_halo(): lax.ppermute(head, axis, [((i + 1) % count, i) for i in range(ends)])]
    unnamed x28 -> x19, local copies, waits for them, and re-layouts: 1.6 us -> 10.2 us
  transfers between devices with their start and end apart: 23 -> 0, of which waited for: 4 -> 0; matrix products, arithmetic and copies ran while one was open for 6% -> 0% of each run, Pallas kernels for 0% -> 0%
where the time goes in v1:
time: 43.4 us; the launch traced here: 43 us
  Pallas kernels  32.1 us (74%)
  local copies, waits for them, and re-layouts  10.2 us (24%)
  between operations  0.66 us (2%)
    pallas_call x1, Pallas kernels, on_device(): pl.pallas_call(kernel, out_shape=(jax.ShapeDtypeStruct((8, 256), F32), fi...  32.1 us
    unnamed x19, local copies, waits for them, and re-layouts  10.2 us

profile of v1, /device:TPU:1, one launch (start us, length us, event | category | flops | bytes accessed | tf_op | source)
XLA Modules:
  0.0 43.0 jit_solution(9648640572432261005)
XLA Ops:
  0.6 0.8 %copy.13.coef = f32[128,32]{1,0:T(8,128)S(1)} copy(f32[128,32]{0,1:T(8,128)} %param.10) | data formatting | bytes 32768 | tf_op args[1]
  1.4 0.0 copy-start
  1.5 1.2 %copy-done = f32[16,128,128]{2,1,0:T(8,128)S(1)} copy-done((f32[16,128,128]{2,1,0:T(8,128)S(1)}, f32[16,128,128]{2,1,0:T(8,128)}, u32[]{:S(2)}) %copy-start) | copy-done | bytes 1048600
  2.7 0.0 copy-start.1
  2.7 0.9 %copy-done.1 = f32[256,256]{1,0:T(8,128)S(1)} copy-done((f32[256,256]{1,0:T(8,128)S(1)}, f32[256,256]{1,0:T(8,128)}, u32[]{:S(2)}) %copy-start.1) | copy-done | bytes 262168
  3.6 0.0 copy-start.2
  3.6 0.9 %copy-done.2 = s32[256,256]{1,0:T(8,128)S(1)} copy-done((s32[256,256]{1,0:T(8,128)S(1)}, s32[256,256]{1,0:T(8,128)}, u32[]{:S(2)}) %copy-start.2) | copy-done | bytes 262168
  4.6 0.0 copy-start.3
  4.6 0.9 %copy-done.3 = f32[256,256]{1,0:T(8,128)S(1)} copy-done((f32[256,256]{1,0:T(8,128)S(1)}, f32[256,256]{1,0:T(8,128)}, u32[]{:S(2)}) %copy-start.3) | copy-done | bytes 262168
  5.5 0.0 copy-start.4
  5.5 0.9 %copy-done.4 = f32[256,256]{1,0:T(8,128)S(1)} copy-done((f32[256,256]{1,0:T(8,128)S(1)}, f32[256,256]{1,0:T(8,128)}, u32[]{:S(2)}) %copy-start.4) | copy-done | bytes 262168
  6.5 0.0 copy-start.5
  6.5 0.9 %copy-done.5 = f32[256,256]{1,0:T(8,128)S(1)} copy-done((f32[256,256]{1,0:T(8,128)S(1)}, f32[256,256]{1,0:T(8,128)}, u32[]{:S(2)}) %copy-start.5) | copy-done | bytes 262168
  7.4 0.0 copy-start.6
  7.4 0.7 %copy-done.6 = s32[4096]{0:T(1024)S(1)} copy-done((s32[4096]{0:T(1024)S(1)}, s32[4096]{0:T(1024)}, u32[]{:S(2)}) %copy-start.6) | copy-done | bytes 16408
  8.1 32.1 %shard_map.120 = (f32[8,256]{1,0:T(8,128)S(1)}, f32[256,256]{1,0:T(8,128)S(1)}, f32[256,256]{1,0:T(8,128)S(1)}, f32[256,256]{1,0:T(8,128)S(1)}) custom-call(bf16[1024,4096]{1,0:T(8,128)(2,1)} %bitcast.3, f32[128,32]{1,0:T(8,128)S(1)} %copy.13.coef, f32[256,256]{1,0:T(8,128)S(1)} %copy-done.1, s32[256,256]{1,0:T(8,128)S(1)} %copy-done.2, ...), custom_call_target="tpu_custom_call" | custom-call | tf_op jit(solution)/shard_map/pallas_call | solution.py:395
  40.3 0.6 %copy.18 = f32[8,256]{1,0:T(8,128)} copy(f32[8,256]{1,0:T(8,128)S(1)} %get-tuple-element.8) | data formatting | bytes 16384
  40.9 0.7 %copy.19 = f32[256,256]{1,0:T(8,128)} copy(f32[256,256]{1,0:T(8,128)S(1)} %get-tuple-element.9) | data formatting | bytes 524288
  41.6 0.7 %copy.20 = f32[256,256]{1,0:T(8,128)} copy(f32[256,256]{1,0:T(8,128)S(1)} %get-tuple-element.10) | data formatting | bytes 524288
  42.3 0.7 %copy.21 = f32[256,256]{1,0:T(8,128)} copy(f32[256,256]{1,0:T(8,128)S(1)} %get-tuple-element.11) | data formatting | bytes 524288
Async XLA Ops:
  1.4 1.2 %copy-start = (f32[16,128,128]{2,1,0:T(8,128)S(1)}, f32[16,128,128]{2,1,0:T(8,128)}, u32[]{:S(2)}) copy-start(f32[16,128,128]{2,1,0:T(8,128)} %constant.2.clone.table) | copy-start | bytes 3145732
  2.7 0.9 %copy-start.1 = (f32[256,256]{1,0:T(8,128)S(1)}, f32[256,256]{1,0:T(8,128)}, u32[]{:S(2)}) copy-start(f32[256,256]{1,0:T(8,128)} %speed.1) | copy-start | bytes 786436
  3.6 0.9 %copy-start.2 = (s32[256,256]{1,0:T(8,128)S(1)}, s32[256,256]{1,0:T(8,128)}, u32[]{:S(2)}) copy-start(s32[256,256]{1,0:T(8,128)} %mask.1) | copy-start | bytes 786436
  4.6 0.9 %copy-start.3 = (f32[256,256]{1,0:T(8,128)S(1)}, f32[256,256]{1,0:T(8,128)}, u32[]{:S(2)}) copy-start(f32[256,256]{1,0:T(8,128)} %surf.1) | copy-start | bytes 786436
  5.5 0.9 %copy-start.4 = (f32[256,256]{1,0:T(8,128)S(1)}, f32[256,256]{1,0:T(8,128)}, u32[]{:S(2)}) copy-start(f32[256,256]{1,0:T(8,128)} %flow_x.1) | copy-start | bytes 786436
  6.5 0.9 %copy-start.5 = (f32[256,256]{1,0:T(8,128)S(1)}, f32[256,256]{1,0:T(8,128)}, u32[]{:S(2)}) copy-start(f32[256,256]{1,0:T(8,128)} %flow_y.1) | copy-start | bytes 786436
  7.4 0.7 %copy-start.6 = (s32[4096]{0:T(1024)S(1)}, s32[4096]{0:T(1024)}, u32[]{:S(2)}) copy-start(s32[4096]{0:T(1024)} %param.13) | copy-start | bytes 49156

commit v2 on v0

v2 whole, which is shorter than its diff:
```python
import functools

import jax
import jax.numpy as jnp
import numpy as np
from jax import lax
from jax.experimental import pallas as pl
from jax.experimental.pallas import tpu as pltpu
from jax.sharding import PartitionSpec as P

F32 = jnp.float32
BF16 = jnp.bfloat16
HIGH = lax.Precision.HIGHEST
MESH = pl.DeviceIdType.MESH
ORDER = (2, 1, 3, 0)


def transform_tables():
    table = np.zeros((16, 128, 128), np.float32)
    times = np.arange(128)
    inner = times.reshape(4, 4, 8).transpose(1, 0, 2).reshape(-1)
    for row in range(16):
        freqs = row * 16 + np.arange(16)
        angle = 2.0 * np.pi * ((freqs[:, None] * inner[None, :]) % 256) / 256.0
        table[row, 0:16] = np.cos(angle) / 256.0
        table[row, 16:32] = -np.sin(angle) / 256.0
        angle = 2.0 * np.pi * ((freqs[:, None] * times[None, :]) % 256) / 256.0
        table[row, 32:48] = np.cos(angle)
        table[row, 48:64] = -np.sin(angle)
        table[row, 64:80] = np.sin(angle)
        table[row, 80:96] = np.cos(angle)
    return table


def after(values, axis):
    return pltpu.roll(values, values.shape[axis] - 1, axis)


def before(values, axis):
    return pltpu.roll(values, 1, axis)


def face_terms(speed, wet):
    celerity = jnp.sqrt(speed)
    terms = []
    for axis in (1, 0):
        opened = wet * after(wet, axis)
        terms.append((0.5 * opened, opened * (0.25 * (celerity + after(celerity, axis)))))
    return terms


def advance(surface, along_x, along_y, speed, wet, terms):
    pressure = speed * surface
    changes = []
    for axis, along, across in ((1, along_x, along_y), (0, along_y, along_x)):
        half, damp = terms[1 - axis]
        next_along = after(along, axis)
        mass = half * (along + next_along) - damp * (after(surface, axis) - surface)
        push = half * (pressure + after(pressure, axis)) - damp * (next_along - along)
        shear = damp * (across - after(across, axis))
        changes.append(tuple(flux - before(flux, axis) for flux in (mass, push, shear)))
    (mass_x, push_x, shear_x), (mass_y, push_y, shear_y) = changes
    return (
        wet * (surface - 0.25 * (mass_x + mass_y)),
        wet * (along_x - 0.25 * (push_x + shear_y)),
        wet * (along_y - 0.25 * (shear_x + push_y)),
    )


def kernel(
    kern, coef, speed, mask, cells, surf, flow_x, flow_y, table,
    series_o, surf_o, flow_x_o, flow_y_o,
    kbuf, tab, cbuf, mbuf, cellbuf, left, own, dsend, drecv, ysend, yrecv,
    xsend, xrecv, zsend, zrecv, gsend, grecv, fields, ewsend, ewrecv, onehot, latest,
    ksem, lsem, dsem, ysem, xsem, zsem, gssem, grsem, nssem, ewsem,
):
    row, col = lax.axis_index("rows"), lax.axis_index("cols")
    x, z_lo = row % 4, row // 4
    y, z_hi, core = col // 4, (col // 2) % 2, col % 2
    z = z_hi * 4 + z_lo
    is_edge = row == 15

    def place(at_x, at_y, at_z, at_core):
        return ((at_z % 4) * 4 + at_x, at_y * 4 + (at_z // 4) * 2 + at_core)

    partner = place(x, y, z, 1 - core)
    y_peer = [place(x, (y + d) % 4, z, core) for d in range(4)]
    x_peer = [place((x + d) % 4, y, z, core) for d in range(4)]
    z_peer = [place(x, y, (z + d) % 8, core) for d in range(8)]
    north, south = ((row + 15) % 16, col), ((row + 1) % 16, col)
    west, east = (row, (col + 15) % 16), (row, (col + 1) % 16)

    with jax.named_scope("greet_peers"):
        barrier = pltpu.get_barrier_semaphore()
        for peer in [partner, *y_peer[1:], *x_peer[1:], *z_peer[1:], north, south, west, east]:
            pl.semaphore_signal(barrier, inc=1, device_id=peer, device_id_type=MESH)

        @pl.when(is_edge)
        def _():
            def greet(index, carry):
                at_z, at_col = index // 8, index % 8
                peer = place(3, at_col // 2, at_z, at_col % 2)

                @pl.when((peer[0] != row) | (peer[1] != col))
                def _():
                    pl.semaphore_signal(barrier, inc=1, device_id=peer, device_id_type=MESH)

                return carry

            lax.fori_loop(0, 64, greet, 0)

    with jax.named_scope("start_loads"):
        local = [
            pltpu.make_async_copy(table.at[row], tab, lsem.at[0]),
            pltpu.make_async_copy(coef, cbuf, lsem.at[1]),
        ]
        for copy in local:
            copy.start()
        loads = []
        for i, d in enumerate(ORDER):
            for side, par in enumerate((1 - core, core)):
                for part in range(2):
                    slot = i * 4 + side * 2 + part
                    start = pl.multiple_of(((((y + d) % 4) * 2 + part) * 2 + par) * 256, 256)
                    copy = pltpu.make_async_copy(
                        kern.at[:, pl.ds(start, 256)], kbuf.at[slot], ksem.at[slot]
                    )
                    copy.start()
                    loads.append(copy)
        inner = (pl.ds(8, 256), pl.ds(0, 256))
        grids = [
            pltpu.make_async_copy(ref, fields.at[(j, *inner)], lsem.at[2 + j])
            for j, ref in enumerate((surf, flow_x, flow_y, speed))
        ]
        grids += [
            pltpu.make_async_copy(mask, mbuf, lsem.at[6]),
            pltpu.make_async_copy(cells, cellbuf, lsem.at[7]),
        ]
        for copy in grids:
            copy.start()

    with jax.named_scope("build_left"):
        for copy in local:
            copy.wait()
        tables = tab[...]
        coefs = lax.dot_general(
            tables[32:96], cbuf[...], (((1,), (1,)), ((), ())),
            precision=HIGH, preferred_element_type=F32,
        )
        lanes = lax.broadcasted_iota(jnp.int32, (32, 512), 1)
        subs = lax.broadcasted_iota(jnp.int32, (32, 512), 0)
        spread = (lanes % 32 == subs).astype(F32).astype(BF16)
        tiled = jnp.dot(coefs.astype(BF16), spread, preferred_element_type=F32)
        diagonal = lanes // 32 == subs % 16
        left[:, 0:512] = jnp.where(diagonal, tiled[0:32], 0.0).astype(BF16)
        left[:, 512:1024] = jnp.where(diagonal, tiled[32:64], 0.0).astype(BF16)

        dcopy, ycopy = [], {}

        def merge(i):
            d = ORDER[i]
            dcopy[i].wait_recv()
            total = own[i] + drecv[i]
            if d == 0:
                own[i] = total
                return
            ysend[d - 1] = total
            ycopy[d] = pltpu.make_async_remote_copy(
                src_ref=ysend.at[d - 1], dst_ref=yrecv.at[d - 1],
                send_sem=ysem.at[0, d - 1], recv_sem=ysem.at[1, d - 1],
                device_id=y_peer[d], device_id_type=MESH,
            )
            ycopy[d].start()

    with jax.named_scope("spectrum"):
        for i in range(4):
            for side in range(2):
                for part in range(2):
                    slot = i * 4 + side * 2 + part
                    loads[slot].wait()
                    spec = jnp.dot(left[...], kbuf[slot], preferred_element_type=F32)
                    target = own if side else dsend
                    target[i, :, part * 256 : part * 256 + 256] = spec
                if side == 0:
                    if i == 0:
                        pl.semaphore_wait(
                            barrier, 18 + jnp.where(x == 3, 16 - is_edge.astype(jnp.int32), 0)
                        )
                    copy = pltpu.make_async_remote_copy(
                        src_ref=dsend.at[i], dst_ref=drecv.at[i],
                        send_sem=dsem.at[0, i], recv_sem=dsem.at[1, i],
                        device_id=partner, device_id_type=MESH,
                    )
                    copy.start()
                    dcopy.append(copy)
            if i >= 1:
                merge(i - 1)

    with jax.named_scope("row_halos"):
        for copy in grids:
            copy.wait()
        fields[(4, *inner)] = mbuf[...].astype(F32)
        ns_copies = []
        for at, (first, last, peer) in enumerate(((8, 264, north), (256, 0, south))):
            copy = pltpu.make_async_remote_copy(
                src_ref=fields.at[:, pl.ds(first, 8), pl.ds(0, 256)],
                dst_ref=fields.at[:, pl.ds(last, 8), pl.ds(0, 256)],
                send_sem=nssem.at[0, at], recv_sem=nssem.at[1, at],
                device_id=peer, device_id_type=MESH,
            )
            copy.start()
            ns_copies.append(copy)
        merge(3)

    with jax.named_scope("selection"):
        def select(block, carry):
            at = lax.broadcasted_iota(jnp.int32, (384, 128), 0)
            column = col * 256 + jnp.where(at >= 320, at - 384, at)
            found = cellbuf[pl.ds(block, 1), :] == column
            onehot[:, pl.ds(pl.multiple_of(block * 128, 128), 128)] = jnp.where(
                found, 1.0, 0.0
            ).astype(BF16)
            return carry

        @pl.when(is_edge)
        def _():
            lax.fori_loop(0, 32, select, 0)

    with jax.named_scope("column_halos"):
        for copy in ns_copies:
            copy.wait_recv()

        @pl.when(row == 0)
        def _():
            fields[:, 0:8, 0:256] = jnp.zeros((5, 8, 256), F32)

        @pl.when(is_edge)
        def _():
            fields[:, 264:272, 0:256] = jnp.zeros((5, 8, 256), F32)

        lane = lax.broadcasted_iota(jnp.int32, (272, 128), 1)
        ew_copies = []
        for at, (first, shift, peer) in enumerate(((0, 0, west), (128, 2, east))):
            packed = jnp.zeros((272, 128), F32)
            for j in range(5):
                block = fields[j, :, first : first + 128]
                if 2 * j + shift:
                    block = pltpu.roll(block, 2 * j + shift, 1)
                packed = jnp.where(lane // 2 == j, block, packed)
            packed = jnp.concatenate([packed, jnp.zeros((112, 128), F32)], axis=0)
            ewsend[at] = packed.T[0:16]
            copy = pltpu.make_async_remote_copy(
                src_ref=ewsend.at[at], dst_ref=ewrecv.at[at],
                send_sem=ewsem.at[0, at], recv_sem=ewsem.at[1, at],
                device_id=peer, device_id_type=MESH,
            )
            copy.start()
            ew_copies.append(copy)

    with jax.named_scope("sum_y"):
        total = own[3]
        for d in (1, 3, 2):
            ycopy[d].wait_recv()
            total = total + yrecv[d - 1]
        inverse = tables.T[:, 0:32]
        partial = jnp.dot(inverse, total, precision=HIGH, preferred_element_type=F32)
        for at in range(4):
            xsend[at] = partial[at * 32 : at * 32 + 32]
        xcopy = {}
        for d in (2, 1, 3):
            xcopy[d] = pltpu.make_async_remote_copy(
                src_ref=xsend.at[(x + d) % 4], dst_ref=xrecv.at[d - 1],
                send_sem=xsem.at[0, d - 1], recv_sem=xsem.at[1, d - 1],
                device_id=x_peer[d], device_id_type=MESH,
            )
            xcopy[d].start()

    with jax.named_scope("place_halos"):
        for copy in ew_copies:
            copy.wait_recv()
        sides = []
        for at, end in ((0, 15), (1, 0)):
            message = jnp.where(col == end, 0.0, ewrecv[at])
            padded = jnp.concatenate([message, jnp.zeros((112, 384), F32)], axis=0)
            sides.append(padded.T[0:272])
        for j in range(5):
            right = pltpu.roll(sides[0], 128 - 2 * j, 1) if j else sides[0]
            wrapped = pltpu.roll(sides[1], 126 - 2 * j, 1)
            fields[j, :, 256:384] = jnp.where(
                lane < 2, right, jnp.where(lane >= 126, wrapped, 0.0)
            )

    with jax.named_scope("sum_x"):
        total = xsend[x]
        for d in (1, 3, 2):
            xcopy[d].wait_recv()
            total = total + xrecv[d - 1]
        zsend[0] = total[:, 0:256]
        zsend[1] = total[:, 256:512]
        gsend[...] = total[30:32]
        me = z * 8 + y * 2 + core

        def ghost_copy(index):
            return pltpu.make_async_remote_copy(
                src_ref=gsend, dst_ref=grecv.at[me],
                send_sem=gssem.at[index], recv_sem=grsem,
                device_id=(15, index), device_id_type=MESH,
            )

        @pl.when(x == 3)
        def _():
            def send(index, carry):
                @pl.when((row != 15) | (index != col))
                def _():
                    ghost_copy(index).start()

                return carry

            lax.fori_loop(0, 16, send, 0)

        zcopy = {}
        for d in (4, 3, 5, 2, 6, 1, 7):
            to = (z + d) % 8
            zcopy[d] = pltpu.make_async_remote_copy(
                src_ref=zsend.at[to // 4, pl.ds(pl.multiple_of((to % 4) * 8, 8), 8)],
                dst_ref=zrecv.at[d - 1],
                send_sem=zsem.at[0, d - 1], recv_sem=zsem.at[1, d - 1],
                device_id=z_peer[d], device_id_type=MESH,
            )
            zcopy[d].start()

    with jax.named_scope("water"):
        def strip(at, carry):
            base = pl.multiple_of(at * 32, 8)
            state = [fields[j, pl.ds(base, 48), :] for j in range(5)]
            values, rest = state[0:3], state[3:5]
            terms = face_terms(*rest)
            for _ in range(2):
                values = advance(*values, *rest, terms)
            for ref, value in zip((surf_o, flow_x_o, flow_y_o), values):
                ref[pl.ds(base, 32), :] = value[8:40, 0:256]
            return carry

        lax.fori_loop(0, 8, strip, 0)

    with jax.named_scope("sum_z"):
        total = zsend[z_hi, pl.ds(pl.multiple_of(z_lo * 8, 8), 8)]
        for d in range(1, 8):
            zcopy[d].wait_recv()
            total = total + zrecv[d - 1]
        series_o[...] = total

    with jax.named_scope("ghost"):
        @pl.when(is_edge)
        def _():
            grecv[me] = gsend[...]
            pltpu.make_async_copy(grecv.at[pl.ds(0, 63)], grecv.at[pl.ds(0, 63)], grsem).wait()
            latest[...] = jnp.zeros((8, 4096), F32)
            for at in range(8):
                summed = grecv[at]
                for other in range(1, 8):
                    summed = summed + grecv[other * 8 + at]
                for part in range(2):
                    first = ((at // 2 * 2 + part) * 2 + at % 2) * 256
                    latest[0:2, first : first + 256] = summed[:, part * 256 : part * 256 + 256]
            value = latest[...]
            high = value.astype(BF16)
            value = value - high.astype(F32)
            middle = value.astype(BF16)
            low = (value - middle.astype(F32)).astype(BF16)
            ghost = jnp.zeros((8, 384), F32)
            for piece in (low, middle, high):
                ghost = ghost + lax.dot_general(
                    piece, onehot[...], (((1,), (1,)), ((), ())), preferred_element_type=F32
                )
            beyond = lax.broadcasted_iota(jnp.int32, (24, 384), 0) == 16
            state = [fields[j, 248:272, :] for j in range(5)]
            rest = [jnp.where(beyond, 1.0, value) for value in state[3:5]]
            values = state[0:3]
            terms = face_terms(*rest)
            for step in range(2):
                values = [
                    jnp.where(beyond, ghost[step : step + 1], values[0]),
                    jnp.where(beyond, 0.0, values[1]),
                    jnp.where(beyond, 0.0, values[2]),
                ]
                values = advance(*values, *rest, terms)
            for ref, value in zip((surf_o, flow_x_o, flow_y_o), values):
                ref[248:256, :] = value[8:16, 0:256]

    with jax.named_scope("drain"):
        for copy in [*dcopy, *ycopy.values(), *xcopy.values(), *zcopy.values(), *ns_copies, *ew_copies]:
            copy.wait_send()

        @pl.when(x == 3)
        def _():
            def finish(index, carry):
                @pl.when((row != 15) | (index != col))
                def _():
                    ghost_copy(index).wait_send()

                return carry

            lax.fori_loop(0, 16, finish, 0)


def write_out(*refs):
    sources, targets, sems = refs[0:4], refs[4:8], refs[8]
    copies = [
        pltpu.make_async_copy(source, target, sems.at[j])
        for j, (source, target) in enumerate(zip(sources, targets))
    ]
    for copy in copies:
        copy.start()
    for copy in copies:
        copy.wait()


def on_device(
    kernel_hat, coefficients, wave_speed_sq, wet_mask, boundary_cell, height, flux_x, flux_y
):
    field = jax.ShapeDtypeStruct((256, 256), F32)
    dma = pltpu.SemaphoreType.DMA
    shapes = (jax.ShapeDtypeStruct((8, 256), F32), field, field, field)
    operands = [
        pltpu.with_memory_space_constraint(value, pltpu.MemorySpace.HBM)
        for value in (
            kernel_hat.reshape(1024, 4096),
            coefficients.T,
            wave_speed_sq,
            wet_mask,
            boundary_cell.reshape(32, 128),
            height,
            flux_x,
            flux_y,
            jnp.asarray(transform_tables()),
        )
    ]
    results = pl.pallas_call(
        kernel,
        out_shape=shapes,
        in_specs=[pl.BlockSpec(memory_space=pltpu.MemorySpace.HBM)] * 9,
        out_specs=[pl.BlockSpec(memory_space=pltpu.VMEM)] * 4,
        scratch_shapes=[
            pltpu.VMEM((16, 1024, 256), BF16),
            pltpu.VMEM((128, 128), F32),
            pltpu.VMEM((32, 128), F32),
            pltpu.VMEM((256, 256), jnp.int32),
            pltpu.VMEM((32, 128), jnp.int32),
            pltpu.VMEM((32, 1024), BF16),
            pltpu.VMEM((4, 32, 512), F32),
            pltpu.VMEM((4, 32, 512), F32),
            pltpu.VMEM((4, 32, 512), F32),
            pltpu.VMEM((3, 32, 512), F32),
            pltpu.VMEM((3, 32, 512), F32),
            pltpu.VMEM((4, 32, 512), F32),
            pltpu.VMEM((3, 32, 512), F32),
            pltpu.VMEM((2, 32, 256), F32),
            pltpu.VMEM((7, 8, 256), F32),
            pltpu.VMEM((2, 512), F32),
            pltpu.VMEM((64, 2, 512), F32),
            pltpu.VMEM((5, 272, 384), F32),
            pltpu.VMEM((2, 16, 384), F32),
            pltpu.VMEM((2, 16, 384), F32),
            pltpu.VMEM((384, 4096), BF16),
            pltpu.VMEM((8, 4096), F32),
            dma((16,)),
            dma((8,)),
            dma((2, 4)),
            dma((2, 3)),
            dma((2, 3)),
            dma((2, 7)),
            dma((16,)),
            dma(()),
            dma((2, 2)),
            dma((2, 2)),
        ],
        compiler_params=pltpu.CompilerParams(
            collective_id=0, has_side_effects=True, vmem_limit_bytes=48 * 1024 * 1024
        ),
    )(*operands)
    return pl.pallas_call(
        write_out,
        out_shape=shapes,
        in_specs=[pl.BlockSpec(memory_space=pltpu.VMEM)] * 4,
        out_specs=[pl.BlockSpec(memory_space=pltpu.MemorySpace.HBM)] * 4,
        scratch_shapes=[dma((4,))],
        compiler_params=pltpu.CompilerParams(vmem_limit_bytes=16 * 1024 * 1024),
    )(*results)


def solution(mesh):
    return jax.shard_map(
        on_device,
        mesh=mesh,
        in_specs=(
            P(None, "rows", "cols", None),
            P(None, "cols"),
            P("rows", "cols"),
            P("rows", "cols"),
            P(),
            P("rows", "cols"),
            P("rows", "cols"),
            P("rows", "cols"),
        ),
        out_specs=(P("rows", "cols"), P("rows", "cols"), P("rows", "cols"), P("rows", "cols")),
        check_vma=False,
    )
```

time: 174 us -> 34.2 us (0.20)
  starting transfers between devices: 112 us -> 0 us
  Pallas kernels: 0 us -> 33.5 us
  waiting for transfers between devices: 23.6 us -> 0 us
  other arithmetic: 16.6 us -> 0 us
  matrix products: 12.6 us -> 0 us
  local copies, waits for them, and re-layouts: 7.15 us -> 0 us
    ppermute x20 -> x0, starting transfers between devices: 75.3 us -> none  [the longest x10 59.2 us: with_halo(): lax.ppermute(tail, axis, [(i, (i + 1) % count) for i in range(ends)])]
    all_to_all x3 -> x0, starting transfers between devices: 36.6 us -> none  [the longest x2 27.1 us: summed_on_arrival(): tiles = lax.all_to_all(split_up(x, dim, length), axis, 0, 0, tiled=True)]
    pallas_call x0 -> x2, Pallas kernels: none -> 33.5 us  [the longest x1 32.5 us: on_device(): pl.pallas_call(kernel, out_shape=shapes, in_specs=[pl.BlockSpec(memory_sp...]
    all_to_all x3 -> x0, waiting for transfers between devices: 14.6 us -> none  [the longest x1 8.5 us: copy_for_each(): return lax.all_to_all(copies, axis, split_axis=0, concat_axis=0, tiled=True)]
    mul x10 -> x0, other arithmetic: 12.7 us -> none  [the longest x4 5.47 us: face_fluxes(): opened * (0.5 * (left_sq * left_surf + right_sq * right_surf) - damping *...]
    dot_general x9 -> x0, matrix products: 12.6 us -> none  [the longest x1 3.35 us: on_device(): jnp.einsum(form, kern_im, coef_re, preferred_element_type=jnp.float32)]
    ppermute x20 -> x0, waiting for transfers between devices: 8.98 us -> none  [the longest x10 8.2 us: with_halo(): lax.ppermute(head, axis, [((i + 1) % count, i) for i in range(ends)])]
    concatenate x10 -> x0, other arithmetic: 3.14 us -> none  [with_halo(): jnp.concatenate([lax.ppermute(tail, axis, [(i, (i + 1) % count) for i in...]
  transfers between devices with their start and end apart: 23 -> 0, of which waited for: 4 -> 0; matrix products, arithmetic and copies ran while one was open for 6% -> 0% of each run, Pallas kernels for 0% -> 0%
where the time goes in v2:
time: 34.2 us; the launch traced here: 34.1 us
  Pallas kernels  33.5 us (98%)
  between operations  0.64 us (2%)
    pallas_call x1, Pallas kernels, on_device(): pl.pallas_call(kernel, out_shape=shapes, in_specs=[pl.BlockSpec(memory_sp...  32.5 us
    pallas_call x1, Pallas kernels, on_device(): pl.pallas_call(write_out, out_shape=shapes, in_specs=[pl.BlockSpec(memory...  0.92 us

profile of v2, /device:TPU:1, one launch (start us, length us, event | category | flops | bytes accessed | tf_op | source)
XLA Modules:
  0.0 34.1 jit_solution(16073521535886676133)
XLA Ops:
  0.6 32.5 %shard_map.120 = (f32[8,256]{1,0:T(8,128)S(1)}, f32[256,256]{1,0:T(8,128)S(1)}, f32[256,256]{1,0:T(8,128)S(1)}, f32[256,256]{1,0:T(8,128)S(1)}) custom-call(bf16[1024,4096]{1,0:T(8,128)(2,1)} %bitcast.3, f32[32,128]{1,0:T(8,128)} %bitcast.4, f32[256,256]{1,0:T(8,128)} %speed.1, s32[256,256]{1,0:T(8,128)} %mask.1, s32[32,128]{1,0:T(8,128)} %bitcast.5, ...), custom_call_target="tpu_custom_call" | custom-call | tf_op jit(solution)/shard_map/pallas_call | solution.py:439
  33.2 0.9 %shard_map.121 = (f32[8,256]{1,0:T(8,128)}, f32[256,256]{1,0:T(8,128)}, f32[256,256]{1,0:T(8,128)}, f32[256,256]{1,0:T(8,128)}) custom-call(f32[8,256]{1,0:T(8,128)S(1)} %get-tuple-element.8.refs_0_, f32[256,256]{1,0:T(8,128)S(1)} %get-tuple-element.9.refs_1_, f32[256,256]{1,0:T(8,128)S(1)} %get-tuple-element.10.refs_2_, ...), custom_call_target="tpu_custom_call" | custom-call | tf_op jit(solution)/shard_map/pallas_call | solution.py:482

commit v3 on v2

--- a/solution.py
+++ b/solution.py
@@ -13,6 +13,7 @@
 HIGH = lax.Precision.HIGHEST
 MESH = pl.DeviceIdType.MESH
 ORDER = (2, 1, 3, 0)
+LOADS = (0, 1, 4, 5, 2, 3, 8, 9, 6, 7, 12, 13, 10, 11, 14, 15)
 
 
 def transform_tables():
@@ -38,6 +39,13 @@
 
 def before(values, axis):
     return pltpu.roll(values, 1, axis)
+
+
+def split_rows(value):
+    high = value.astype(BF16)
+    value = value - high.astype(F32)
+    middle = value.astype(BF16)
+    return [high, middle, (value - middle.astype(F32)).astype(BF16)]
 
 
 def face_terms(speed, wet):
@@ -71,7 +79,7 @@
     kern, coef, speed, mask, cells, surf, flow_x, flow_y, table,
     series_o, surf_o, flow_x_o, flow_y_o,
     kbuf, tab, cbuf, mbuf, cellbuf, left, own, dsend, drecv, ysend, yrecv,
-    xsend, xrecv, zsend, zrecv, gsend, grecv, fields, ewsend, ewrecv, onehot, latest,
+    xsend, xrecv, zsend, zrecv, gsend, grecv, fields, ewsend, ewrecv, onehot, blocks, wide,
     ksem, lsem, dsem, ysem, xsem, zsem, gssem, grsem, nssem, ewsem,
 ):
     row, col = lax.axis_index("rows"), lax.axis_index("cols")
@@ -90,43 +98,25 @@
     north, south = ((row + 15) % 16, col), ((row + 1) % 16, col)
     west, east = (row, (col + 15) % 16), (row, (col + 1) % 16)
 
-    with jax.named_scope("greet_peers"):
-        barrier = pltpu.get_barrier_semaphore()
-        for peer in [partner, *y_peer[1:], *x_peer[1:], *z_peer[1:], north, south, west, east]:
-            pl.semaphore_signal(barrier, inc=1, device_id=peer, device_id_type=MESH)
-
-        @pl.when(is_edge)
-        def _():
-            def greet(index, carry):
-                at_z, at_col = index // 8, index % 8
-                peer = place(3, at_col // 2, at_z, at_col % 2)
-
-                @pl.when((peer[0] != row) | (peer[1] != col))
-                def _():
-                    pl.semaphore_signal(barrier, inc=1, device_id=peer, device_id_type=MESH)
-
-                return carry
-
-            lax.fori_loop(0, 64, greet, 0)
-
     with jax.named_scope("start_loads"):
-        local = [
-            pltpu.make_async_copy(table.at[row], tab, lsem.at[0]),
-            pltpu.make_async_copy(coef, cbuf, lsem.at[1]),
-        ]
-        for copy in local:
-            copy.start()
+        local = [pltpu.make_async_copy(table.at[row], tab, lsem.at[0])]
+        local[0].start()
+        for i in range(16):
+            pltpu.make_async_copy(coef, cbuf.at[pl.ds(i * 32, 32)], lsem.at[1]).start()
+        local.append(pltpu.make_async_copy(cbuf, cbuf, lsem.at[1]))
         loads = []
         for i, d in enumerate(ORDER):
             for side, par in enumerate((1 - core, core)):
                 for part in range(2):
                     slot = i * 4 + side * 2 + part
                     start = pl.multiple_of(((((y + d) % 4) * 2 + part) * 2 + par) * 256, 256)
-                    copy = pltpu.make_async_copy(
-                        kern.at[:, pl.ds(start, 256)], kbuf.at[slot], ksem.at[slot]
+                    loads.append(
+                        pltpu.make_async_copy(
+                            kern.at[:, pl.ds(start, 256)], kbuf.at[slot], ksem.at[slot]
+                        )
                     )
-                    copy.start()
-                    loads.append(copy)
+        for slot in LOADS:
+            loads[slot].start()
         inner = (pl.ds(8, 256), pl.ds(0, 256))
         grids = [
             pltpu.make_async_copy(ref, fields.at[(j, *inner)], lsem.at[2 + j])
@@ -139,23 +129,63 @@
         for copy in grids:
             copy.start()
 
+    with jax.named_scope("greet_peers"):
+        barrier = pltpu.get_barrier_semaphore()
+        for peer in [partner, *y_peer[1:], *x_peer[1:], *z_peer[1:], north, south, west, east]:
+            pl.semaphore_signal(barrier, inc=1, device_id=peer, device_id_type=MESH)
+
+        @pl.when(is_edge)
+        def _():
+            for at_row in (3, 7, 11, 15):
+                for at_col in range(16):
+                    def greet(peer=(at_row, at_col)):
+                        pl.semaphore_signal(barrier, inc=1, device_id=peer, device_id_type=MESH)
+
+                    if at_row == 15:
+                        pl.when(col != at_col)(greet)
+                    else:
+                        greet()
+
     with jax.named_scope("build_left"):
         for copy in local:
             copy.wait()
         tables = tab[...]
-        coefs = lax.dot_general(
+        tiled = lax.dot_general(
             tables[32:96], cbuf[...], (((1,), (1,)), ((), ())),
             precision=HIGH, preferred_element_type=F32,
         )
         lanes = lax.broadcasted_iota(jnp.int32, (32, 512), 1)
         subs = lax.broadcasted_iota(jnp.int32, (32, 512), 0)
-        spread = (lanes % 32 == subs).astype(F32).astype(BF16)
-        tiled = jnp.dot(coefs.astype(BF16), spread, preferred_element_type=F32)
-        diagonal = lanes // 32 == subs % 16
+        diagonal = (lanes >> 5) == (subs & 15)
         left[:, 0:512] = jnp.where(diagonal, tiled[0:32], 0.0).astype(BF16)
         left[:, 512:1024] = jnp.where(diagonal, tiled[32:64], 0.0).astype(BF16)
 
         dcopy, ycopy = [], {}
+
+        def part_of(i, side, target):
+            for part in range(2):
+                slot = i * 4 + side * 2 + part
+                loads[slot].wait()
+                target[i, :, part * 256 : part * 256 + 256] = jnp.dot(
+                    left[...], kbuf[slot], preferred_element_type=F32
+                )
+
+        def other(i):
+            part_of(i, 0, dsend)
+            if i == 0:
+                pl.semaphore_wait(
+                    barrier, 18 + jnp.where(x == 3, 16 - is_edge.astype(jnp.int32), 0)
+                )
+            copy = pltpu.make_async_remote_copy(
+                src_ref=dsend.at[i], dst_ref=drecv.at[i],
+                send_sem=dsem.at[0, i], recv_sem=dsem.at[1, i],
+                device_id=partner, device_id_type=MESH,
+            )
+            copy.start()
+            dcopy.append(copy)
+
+        def mine(i):
+            part_of(i, 1, own)
 
         def merge(i):
             d = ORDER[i]
@@ -173,28 +203,17 @@
             ycopy[d].start()
 
     with jax.named_scope("spectrum"):
-        for i in range(4):
-            for side in range(2):
-                for part in range(2):
-                    slot = i * 4 + side * 2 + part
-                    loads[slot].wait()
-                    spec = jnp.dot(left[...], kbuf[slot], preferred_element_type=F32)
-                    target = own if side else dsend
-                    target[i, :, part * 256 : part * 256 + 256] = spec
-                if side == 0:
-                    if i == 0:
-                        pl.semaphore_wait(
-                            barrier, 18 + jnp.where(x == 3, 16 - is_edge.astype(jnp.int32), 0)
-                        )
-                    copy = pltpu.make_async_remote_copy(
-                        src_ref=dsend.at[i], dst_ref=drecv.at[i],
-                        send_sem=dsem.at[0, i], recv_sem=dsem.at[1, i],
-                        device_id=partner, device_id_type=MESH,
-                    )
-                    copy.start()
-                    dcopy.append(copy)
-            if i >= 1:
-                merge(i - 1)
+        other(0)
+        other(1)
+        mine(0)
+        other(2)
+        mine(1)
+        merge(0)
+        other(3)
+        mine(2)
+        merge(1)
+        mine(3)
+        merge(2)
 
     with jax.named_scope("row_halos"):
         for copy in grids:
@@ -210,21 +229,30 @@
             )
             copy.start()
             ns_copies.append(copy)
+        split = split_rows(tables[0:32])
+        wide[...] = jnp.concatenate(
+            [*(split[k].astype(F32) for k in (0, 0, 1, 0, 2, 1)), jnp.zeros((64, 128), F32)], axis=0
+        ).T.astype(BF16)
         merge(3)
 
-    with jax.named_scope("selection"):
-        def select(block, carry):
-            at = lax.broadcasted_iota(jnp.int32, (384, 128), 0)
-            column = col * 256 + jnp.where(at >= 320, at - 384, at)
-            found = cellbuf[pl.ds(block, 1), :] == column
-            onehot[:, pl.ds(pl.multiple_of(block * 128, 128), 128)] = jnp.where(
-                found, 1.0, 0.0
-            ).astype(BF16)
-            return carry
-
-        @pl.when(is_edge)
-        def _():
-            lax.fori_loop(0, 32, select, 0)
+    with jax.named_scope("sum_y"):
+        total = own[3]
+        for d in (1, 3, 2):
+            ycopy[d].wait_recv()
+            total = total + yrecv[d - 1]
+        split = split_rows(total)
+        stack = jnp.concatenate([split[k] for k in (0, 1, 0, 2, 0, 1)], axis=0)
+        partial = jnp.dot(wide[:, 0:192], stack, preferred_element_type=F32)
+        for at in range(4):
+            xsend[at] = partial[at * 32 : at * 32 + 32]
+        xcopy = {}
+        for d in (2, 1, 3):
+            xcopy[d] = pltpu.make_async_remote_copy(
+                src_ref=xsend.at[(x + d) % 4], dst_ref=xrecv.at[d - 1],
+                send_sem=xsem.at[0, d - 1], recv_sem=xsem.at[1, d - 1],
+                device_id=x_peer[d], device_id_type=MESH,
+            )
+            xcopy[d].start()
 
     with jax.named_scope("column_halos"):
         for copy in ns_copies:
@@ -257,23 +285,53 @@
             copy.start()
             ew_copies.append(copy)
 
-    with jax.named_scope("sum_y"):
-        total = own[3]
+    with jax.named_scope("selection"):
+        @pl.when(is_edge)
+        def _():
+            at = lax.broadcasted_iota(jnp.int32, (128, 384), 1)
+            column = col * 256 + jnp.where(at >= 320, at - 384, at)
+            turned = jnp.concatenate(
+                [cellbuf[...].astype(F32), jnp.zeros((96, 128), F32)], axis=0
+            ).T.astype(jnp.int32)
+            found = jnp.zeros((128, 384), F32)
+            for block in range(32):
+                found = jnp.where(turned[:, block : block + 1] == column, block + 1.0, found)
+            onehot[...] = jnp.where(found > 0.0, 1.0, 0.0).astype(BF16)
+            blocks[...] = jnp.broadcast_to(jnp.sum(found, axis=0, keepdims=True), (8, 384))
+
+    with jax.named_scope("sum_x"):
+        total = xsend[x]
         for d in (1, 3, 2):
-            ycopy[d].wait_recv()
-            total = total + yrecv[d - 1]
-        inverse = tables.T[:, 0:32]
-        partial = jnp.dot(inverse, total, precision=HIGH, preferred_element_type=F32)
-        for at in range(4):
-            xsend[at] = partial[at * 32 : at * 32 + 32]
-        xcopy = {}
-        for d in (2, 1, 3):
-            xcopy[d] = pltpu.make_async_remote_copy(
-                src_ref=xsend.at[(x + d) % 4], dst_ref=xrecv.at[d - 1],
-                send_sem=xsem.at[0, d - 1], recv_sem=xsem.at[1, d - 1],
-                device_id=x_peer[d], device_id_type=MESH,
-            )
-            xcopy[d].start()
+            xcopy[d].wait_recv()
+            total = total + xrecv[d - 1]
+        zsend[0] = total[:, 0:256]
+        zsend[1] = total[:, 256:512]
+        for at in range(8):
+            gsend[at : at + 1] = total[30 + at // 4 : 31 + at // 4, at % 4 * 128 : at % 4 * 128 + 128]
+        here = pl.ds(pl.multiple_of((z * 8 + y * 2 + core) * 8, 8), 8)
+
+        def ghost_copy(index):
+            return pltpu.make_async_remote_copy(
+                src_ref=gsend, dst_ref=grecv.at[here],
+                send_sem=gssem.at[index], recv_sem=grsem,
+                device_id=(15, index), device_id_type=MESH,
+            )
+
+        @pl.when(x == 3)
+        def _():
+            for index in range(16):
+                pl.when((row != 15) | (col != index))(ghost_copy(index).start)
+
+        zcopy = {}
+        for d in (4, 3, 5, 2, 6, 1, 7):
+            to = (z + d) % 8
+            zcopy[d] = pltpu.make_async_remote_copy(
+                src_ref=zsend.at[to // 4, pl.ds(pl.multiple_of((to % 4) * 8, 8), 8)],
+                dst_ref=zrecv.at[d - 1],
+                send_sem=zsem.at[0, d - 1], recv_sem=zsem.at[1, d - 1],
+                device_id=z_peer[d], device_id_type=MESH,
+            )
+            zcopy[d].start()
 
     with jax.named_scope("place_halos"):
         for copy in ew_copies:
@@ -290,45 +348,6 @@
                 lane < 2, right, jnp.where(lane >= 126, wrapped, 0.0)
             )
 
-    with jax.named_scope("sum_x"):
-        total = xsend[x]
-        for d in (1, 3, 2):
-            xcopy[d].wait_recv()
-            total = total + xrecv[d - 1]
-        zsend[0] = total[:, 0:256]
-        zsend[1] = total[:, 256:512]
-        gsend[...] = total[30:32]
-        me = z * 8 + y * 2 + core
-
-        def ghost_copy(index):
-            return pltpu.make_async_remote_copy(
-                src_ref=gsend, dst_ref=grecv.at[me],
-                send_sem=gssem.at[index], recv_sem=grsem,
-                device_id=(15, index), device_id_type=MESH,
-            )
-
-        @pl.when(x == 3)
-        def _():
-            def send(index, carry):
-                @pl.when((row != 15) | (index != col))
-                def _():
-                    ghost_copy(index).start()
-
-                return carry
-
-            lax.fori_loop(0, 16, send, 0)
-
-        zcopy = {}
-        for d in (4, 3, 5, 2, 6, 1, 7):
-            to = (z + d) % 8
-            zcopy[d] = pltpu.make_async_remote_copy(
-                src_ref=zsend.at[to // 4, pl.ds(pl.multiple_of((to % 4) * 8, 8), 8)],
-                dst_ref=zrecv.at[d - 1],
-                send_sem=zsem.at[0, d - 1], recv_sem=zsem.at[1, d - 1],
-                device_id=z_peer[d], device_id_type=MESH,
-            )
-            zcopy[d].start()
-
     with jax.named_scope("water"):
         def strip(at, carry):
             base = pl.multiple_of(at * 32, 8)
@@ -353,26 +372,25 @@
     with jax.named_scope("ghost"):
         @pl.when(is_edge)
         def _():
-            grecv[me] = gsend[...]
-            pltpu.make_async_copy(grecv.at[pl.ds(0, 63)], grecv.at[pl.ds(0, 63)], grsem).wait()
-            latest[...] = jnp.zeros((8, 4096), F32)
-            for at in range(8):
-                summed = grecv[at]
-                for other in range(1, 8):
-                    summed = summed + grecv[other * 8 + at]
-                for part in range(2):
-                    first = ((at // 2 * 2 + part) * 2 + at % 2) * 256
-                    latest[0:2, first : first + 256] = summed[:, part * 256 : part * 256 + 256]
-            value = latest[...]
-            high = value.astype(BF16)
-            value = value - high.astype(F32)
-            middle = value.astype(BF16)
-            low = (value - middle.astype(F32)).astype(BF16)
-            ghost = jnp.zeros((8, 384), F32)
-            for piece in (low, middle, high):
-                ghost = ghost + lax.dot_general(
-                    piece, onehot[...], (((1,), (1,)), ((), ())), preferred_element_type=F32
-                )
+            grecv[here] = gsend[...]
+            pltpu.make_async_copy(
+                grecv.at[pl.ds(0, 504)], grecv.at[pl.ds(0, 504)], grsem
+            ).wait()
+            value = grecv[0:64]
+            for other_z in range(1, 8):
+                value = value + grecv[other_z * 64 : other_z * 64 + 64]
+            picked = jnp.dot(
+                jnp.concatenate(split_rows(value), axis=0), onehot[...],
+                preferred_element_type=F32,
+            )
+            picked = picked[128:192] + picked[64:128] + picked[0:64]
+            at = lax.broadcasted_iota(jnp.int32, (64, 384), 0)
+            block = (at >> 4) * 8 + (at & 2) * 2 + ((at >> 3) & 1) * 2 + (at & 1)
+            picked = jnp.where((block + 1).astype(F32) == blocks[0:1], picked, 0.0)
+            ghost = [
+                jnp.sum(jnp.where(((at >> 2) & 1) == step, picked, 0.0), axis=0, keepdims=True)
+                for step in range(2)
+            ]
             beyond = lax.broadcasted_iota(jnp.int32, (24, 384), 0) == 16
             state = [fields[j, 248:272, :] for j in range(5)]
             rest = [jnp.where(beyond, 1.0, value) for value in state[3:5]]
@@ -380,7 +398,7 @@
             terms = face_terms(*rest)
             for step in range(2):
                 values = [
-                    jnp.where(beyond, ghost[step : step + 1], values[0]),
+                    jnp.where(beyond, ghost[step], values[0]),
                     jnp.where(beyond, 0.0, values[1]),
                     jnp.where(beyond, 0.0, values[2]),
                 ]
@@ -394,14 +412,8 @@
 
         @pl.when(x == 3)
         def _():
-            def finish(index, carry):
-                @pl.when((row != 15) | (index != col))
-                def _():
-                    ghost_copy(index).wait_send()
-
-                return carry
-
-            lax.fori_loop(0, 16, finish, 0)
+            for index in range(16):
+                pl.when((row != 15) | (col != index))(ghost_copy(index).wait_send)
 
 
 def write_out(*refs):
@@ -444,7 +456,7 @@
         scratch_shapes=[
             pltpu.VMEM((16, 1024, 256), BF16),
             pltpu.VMEM((128, 128), F32),
-            pltpu.VMEM((32, 128), F32),
+            pltpu.VMEM((512, 128), F32),
             pltpu.VMEM((256, 256), jnp.int32),
             pltpu.VMEM((32, 128), jnp.int32),
             pltpu.VMEM((32, 1024), BF16),
@@ -457,13 +469,14 @@
             pltpu.VMEM((3, 32, 512), F32),
             pltpu.VMEM((2, 32, 256), F32),
             pltpu.VMEM((7, 8, 256), F32),
-            pltpu.VMEM((2, 512), F32),
-            pltpu.VMEM((64, 2, 512), F32),
+            pltpu.VMEM((8, 128), F32),
+            pltpu.VMEM((512, 128), F32),
             pltpu.VMEM((5, 272, 384), F32),
             pltpu.VMEM((2, 16, 384), F32),
             pltpu.VMEM((2, 16, 384), F32),
-            pltpu.VMEM((384, 4096), BF16),
-            pltpu.VMEM((8, 4096), F32),
+            pltpu.VMEM((128, 384), BF16),
+            pltpu.VMEM((8, 384), F32),
+            pltpu.VMEM((128, 256), BF16),
             dma((16,)),
             dma((8,)),
             dma((2, 4)),

time: 34.2 us -> 32.1 us (0.939)
  Pallas kernels: 33.5 us -> 31.4 us
    pallas_call x1, Pallas kernels: 32.5 us -> 30.5 us  [on_device(): pl.pallas_call(kernel, out_shape=shapes, in_specs=[pl.BlockSpec(memory_sp...]
where the time goes in v3:
time: 32.1 us
  Pallas kernels  31.4 us (98%)
  between operations  0.64 us (2%)
    pallas_call x1, Pallas kernels, on_device(): pl.pallas_call(kernel, out_shape=shapes, in_specs=[pl.BlockSpec(memory_sp...  30.5 us
    pallas_call x1, Pallas kernels, on_device(): pl.pallas_call(write_out, out_shape=shapes, in_specs=[pl.BlockSpec(memory...  0.92 us

profile of v3, /device:TPU:1, one launch (start us, length us, event | category | flops | bytes accessed | tf_op | source)
XLA Modules:
  0.0 32.1 jit_solution(12868622822324280763)
XLA Ops:
  0.6 30.5 %shard_map.120 = (f32[8,256]{1,0:T(8,128)S(1)}, f32[256,256]{1,0:T(8,128)S(1)}, f32[256,256]{1,0:T(8,128)S(1)}, f32[256,256]{1,0:T(8,128)S(1)}) custom-call(bf16[1024,4096]{1,0:T(8,128)(2,1)} %bitcast.3, f32[32,128]{1,0:T(8,128)} %bitcast.4, f32[256,256]{1,0:T(8,128)} %speed.1, s32[256,256]{1,0:T(8,128)} %mask.1, s32[32,128]{1,0:T(8,128)} %bitcast.5, ...), custom_call_target="tpu_custom_call" | custom-call | tf_op jit(solution)/shard_map/pallas_call | solution.py:451
  31.1 0.9 %shard_map.121 = (f32[8,256]{1,0:T(8,128)}, f32[256,256]{1,0:T(8,128)}, f32[256,256]{1,0:T(8,128)}, f32[256,256]{1,0:T(8,128)}) custom-call(f32[8,256]{1,0:T(8,128)S(1)} %get-tuple-element.8.refs_0_, f32[256,256]{1,0:T(8,128)S(1)} %get-tuple-element.9.refs_1_, f32[256,256]{1,0:T(8,128)S(1)} %get-tuple-element.10.refs_2_, ...), custom_call_target="tpu_custom_call" | custom-call | tf_op jit(solution)/shard_map/pallas_call | solution.py:495

commit v4 on v3

--- a/solution.py
+++ b/solution.py
@@ -48,20 +48,21 @@
     return [high, middle, (value - middle.astype(F32)).astype(BF16)]
 
 
-def face_terms(speed, wet):
+def face_terms(speed, wet, axes=(1, 0)):
     celerity = jnp.sqrt(speed)
     terms = []
-    for axis in (1, 0):
+    for axis in axes:
         opened = wet * after(wet, axis)
         terms.append((0.5 * opened, opened * (0.25 * (celerity + after(celerity, axis)))))
     return terms
 
 
-def advance(surface, along_x, along_y, speed, wet, terms):
+def advance(surface, along_x, along_y, speed, wet, terms, axes=(1, 0)):
     pressure = speed * surface
     changes = []
-    for axis, along, across in ((1, along_x, along_y), (0, along_y, along_x)):
-        half, damp = terms[1 - axis]
+    for axis, along, across, (half, damp) in zip(
+        axes, (along_x, along_y), (along_y, along_x), terms
+    ):
         next_along = after(along, axis)
         mass = half * (along + next_along) - damp * (after(surface, axis) - surface)
         push = half * (pressure + after(pressure, axis)) - damp * (next_along - along)
@@ -79,7 +80,7 @@
     kern, coef, speed, mask, cells, surf, flow_x, flow_y, table,
     series_o, surf_o, flow_x_o, flow_y_o,
     kbuf, tab, cbuf, mbuf, cellbuf, left, own, dsend, drecv, ysend, yrecv,
-    xsend, xrecv, zsend, zrecv, gsend, grecv, fields, ewsend, ewrecv, onehot, blocks, wide,
+    xsend, xrecv, zsend, zrecv, gsend, grecv, fields, ewsend, ewrecv, sides, tail, onehot, blocks, wide,
     ksem, lsem, dsem, ysem, xsem, zsem, gssem, grsem, nssem, ewsem,
 ):
     row, col = lax.axis_index("rows"), lax.axis_index("cols")
@@ -101,9 +102,8 @@
     with jax.named_scope("start_loads"):
         local = [pltpu.make_async_copy(table.at[row], tab, lsem.at[0])]
         local[0].start()
-        for i in range(16):
-            pltpu.make_async_copy(coef, cbuf.at[pl.ds(i * 32, 32)], lsem.at[1]).start()
-        local.append(pltpu.make_async_copy(cbuf, cbuf, lsem.at[1]))
+        local.append(pltpu.make_async_copy(coef, cbuf, lsem.at[1]))
+        local[1].start()
         loads = []
         for i, d in enumerate(ORDER):
             for side, par in enumerate((1 - core, core)):
@@ -115,9 +115,9 @@
                             kern.at[:, pl.ds(start, 256)], kbuf.at[slot], ksem.at[slot]
                         )
                     )
-        for slot in LOADS:
+        for slot in LOADS[0:4]:
             loads[slot].start()
-        inner = (pl.ds(8, 256), pl.ds(0, 256))
+        inner = (pl.ds(8, 256), slice(None))
         grids = [
             pltpu.make_async_copy(ref, fields.at[(j, *inner)], lsem.at[2 + j])
             for j, ref in enumerate((surf, flow_x, flow_y, speed))
@@ -128,6 +128,8 @@
         ]
         for copy in grids:
             copy.start()
+        for slot in LOADS[4:]:
+            loads[slot].start()
 
     with jax.named_scope("greet_peers"):
         barrier = pltpu.get_barrier_semaphore()
@@ -151,7 +153,7 @@
             copy.wait()
         tables = tab[...]
         tiled = lax.dot_general(
-            tables[32:96], cbuf[...], (((1,), (1,)), ((), ())),
+            tables[32:96], jnp.concatenate([cbuf[...]] * 16, axis=0), (((1,), (1,)), ((), ())),
             precision=HIGH, preferred_element_type=F32,
         )
         lanes = lax.broadcasted_iota(jnp.int32, (32, 512), 1)
@@ -205,6 +207,20 @@
     with jax.named_scope("spectrum"):
         other(0)
         other(1)
+
+        for copy in grids:
+            copy.wait()
+        fields[(4, *inner)] = mbuf[...].astype(F32)
+        ns_copies = []
+        for at, (first, last, peer) in enumerate(((8, 264, north), (256, 0, south))):
+            copy = pltpu.make_async_remote_copy(
+                src_ref=fields.at[:, pl.ds(first, 8)],
+                dst_ref=fields.at[:, pl.ds(last, 8)],
+                send_sem=nssem.at[0, at], recv_sem=nssem.at[1, at],
+                device_id=peer, device_id_type=MESH,
+            )
+            copy.start()
+            ns_copies.append(copy)
         mine(0)
         other(2)
         mine(1)
@@ -215,25 +231,43 @@
         mine(3)
         merge(2)
 
-    with jax.named_scope("row_halos"):
-        for copy in grids:
-            copy.wait()
-        fields[(4, *inner)] = mbuf[...].astype(F32)
-        ns_copies = []
-        for at, (first, last, peer) in enumerate(((8, 264, north), (256, 0, south))):
-            copy = pltpu.make_async_remote_copy(
-                src_ref=fields.at[:, pl.ds(first, 8), pl.ds(0, 256)],
-                dst_ref=fields.at[:, pl.ds(last, 8), pl.ds(0, 256)],
-                send_sem=nssem.at[0, at], recv_sem=nssem.at[1, at],
-                device_id=peer, device_id_type=MESH,
-            )
-            copy.start()
-            ns_copies.append(copy)
+    with jax.named_scope("widen"):
         split = split_rows(tables[0:32])
         wide[...] = jnp.concatenate(
             [*(split[k].astype(F32) for k in (0, 0, 1, 0, 2, 1)), jnp.zeros((64, 128), F32)], axis=0
         ).T.astype(BF16)
         merge(3)
+
+    with jax.named_scope("column_halos"):
+        for copy in ns_copies:
+            copy.wait_recv()
+
+        @pl.when(row == 0)
+        def _():
+            fields[:, 0:8, :] = jnp.zeros((5, 8, 256), F32)
+
+        @pl.when(is_edge)
+        def _():
+            fields[:, 264:272, :] = jnp.zeros((5, 8, 256), F32)
+
+        lane = lax.broadcasted_iota(jnp.int32, (272, 128), 1)
+        ew_copies = []
+        for at, (first, shift, peer) in enumerate(((0, 0, west), (128, 4, east))):
+            packed = jnp.zeros((272, 128), F32)
+            for j in range(5):
+                block = fields[j, :, first : first + 128]
+                if 4 * j + shift:
+                    block = pltpu.roll(block, 4 * j + shift, 1)
+                packed = jnp.where((lane >> 2) == j, block, packed)
+            packed = jnp.concatenate([packed, jnp.zeros((112, 128), F32)], axis=0)
+            ewsend[at] = packed.T[0:24]
+            copy = pltpu.make_async_remote_copy(
+                src_ref=ewsend.at[at], dst_ref=ewrecv.at[at],
+                send_sem=ewsem.at[0, at], recv_sem=ewsem.at[1, at],
+                device_id=peer, device_id_type=MESH,
+            )
+            copy.start()
+            ew_copies.append(copy)
 
     with jax.named_scope("sum_y"):
         total = own[3]
@@ -254,37 +288,6 @@
             )
             xcopy[d].start()
 
-    with jax.named_scope("column_halos"):
-        for copy in ns_copies:
-            copy.wait_recv()
-
-        @pl.when(row == 0)
-        def _():
-            fields[:, 0:8, 0:256] = jnp.zeros((5, 8, 256), F32)
-
-        @pl.when(is_edge)
-        def _():
-            fields[:, 264:272, 0:256] = jnp.zeros((5, 8, 256), F32)
-
-        lane = lax.broadcasted_iota(jnp.int32, (272, 128), 1)
-        ew_copies = []
-        for at, (first, shift, peer) in enumerate(((0, 0, west), (128, 2, east))):
-            packed = jnp.zeros((272, 128), F32)
-            for j in range(5):
-                block = fields[j, :, first : first + 128]
-                if 2 * j + shift:
-                    block = pltpu.roll(block, 2 * j + shift, 1)
-                packed = jnp.where(lane // 2 == j, block, packed)
-            packed = jnp.concatenate([packed, jnp.zeros((112, 128), F32)], axis=0)
-            ewsend[at] = packed.T[0:16]
-            copy = pltpu.make_async_remote_copy(
-                src_ref=ewsend.at[at], dst_ref=ewrecv.at[at],
-                send_sem=ewsem.at[0, at], recv_sem=ewsem.at[1, at],
-                device_id=peer, device_id_type=MESH,
-            )
-            copy.start()
-            ew_copies.append(copy)
-
     with jax.named_scope("selection"):
         @pl.when(is_edge)
         def _():
@@ -299,6 +302,20 @@
             onehot[...] = jnp.where(found > 0.0, 1.0, 0.0).astype(BF16)
             blocks[...] = jnp.broadcast_to(jnp.sum(found, axis=0, keepdims=True), (8, 384))
 
+    with jax.named_scope("water"):
+        def strip(at, carry):
+            base = pl.multiple_of(at * 32, 8)
+            state = [fields[j, pl.ds(base, 48), :] for j in range(5)]
+            values, rest = state[0:3], state[3:5]
+            terms = face_terms(*rest)
+            for _ in range(2):
+                values = advance(*values, *rest, terms)
+            for ref, value in zip((surf_o, flow_x_o, flow_y_o), values):
+                ref[pl.ds(base, 32), :] = value[8:40]
+            return carry
+
+        lax.fori_loop(0, 8, strip, 0)
+
     with jax.named_scope("sum_x"):
         total = xsend[x]
         for d in (1, 3, 2):
@@ -333,34 +350,41 @@
             )
             zcopy[d].start()
 
-    with jax.named_scope("place_halos"):
+    with jax.named_scope("side_water"):
         for copy in ew_copies:
             copy.wait_recv()
-        sides = []
-        for at, end in ((0, 15), (1, 0)):
-            message = jnp.where(col == end, 0.0, ewrecv[at])
-            padded = jnp.concatenate([message, jnp.zeros((112, 384), F32)], axis=0)
-            sides.append(padded.T[0:272])
+        from_east = jnp.where(col == 15, 0.0, ewrecv[0])
+        from_west = jnp.where(col == 0, 0.0, ewrecv[1])
         for j in range(5):
-            right = pltpu.roll(sides[0], 128 - 2 * j, 1) if j else sides[0]
-            wrapped = pltpu.roll(sides[1], 126 - 2 * j, 1)
-            fields[j, :, 256:384] = jnp.where(
-                lane < 2, right, jnp.where(lane >= 126, wrapped, 0.0)
-            )
-
-    with jax.named_scope("water"):
-        def strip(at, carry):
-            base = pl.multiple_of(at * 32, 8)
-            state = [fields[j, pl.ds(base, 48), :] for j in range(5)]
-            values, rest = state[0:3], state[3:5]
-            terms = face_terms(*rest)
-            for _ in range(2):
-                values = advance(*values, *rest, terms)
-            for ref, value in zip((surf_o, flow_x_o, flow_y_o), values):
-                ref[pl.ds(base, 32), :] = value[8:40, 0:256]
-            return carry
-
-        lax.fori_loop(0, 8, strip, 0)
+            for at, piece in enumerate((from_west, ewsend[0], ewsend[1], from_east)):
+                sides[j, at * 4 : at * 4 + 4] = piece[j * 4 : j * 4 + 4]
+        state = [sides[j] for j in range(5)]
+        values, rest = state[0:3], state[3:5]
+        terms = face_terms(*rest, (0, 1))
+        for _ in range(2):
+            values = advance(*values, *rest, terms, (0, 1))
+        turned = jnp.concatenate([*values, jnp.zeros((80, 384), F32)], axis=0).T[8:264]
+        lane = lax.broadcasted_iota(jnp.int32, (256, 128), 1)
+        for j, ref in enumerate((surf_o, flow_x_o, flow_y_o)):
+            ref[:, 0:128] = jnp.where(
+                lane < 2, pltpu.roll(turned, 124 - 16 * j, 1), ref[:, 0:128]
+            )
+            ref[:, 128:256] = jnp.where(
+                lane >= 126, pltpu.roll(turned, 116 - 16 * j, 1), ref[:, 128:256]
+            )
+
+        @pl.when(is_edge)
+        def _():
+            blank = jnp.zeros((104, 256), F32)
+            right, left_side = (
+                jnp.concatenate([piece[:, 128:384], blank], axis=0).T[120:144]
+                for piece in (from_east, from_west)
+            )
+            lane = lax.broadcasted_iota(jnp.int32, (24, 128), 1)
+            for j in range(5):
+                first = pltpu.roll(right, 128 - 4 * j, 1) if j else right
+                wrapped = pltpu.roll(left_side, 124 - 4 * j, 1)
+                tail[j] = jnp.where(lane < 2, first, jnp.where(lane >= 126, wrapped, 0.0))
 
     with jax.named_scope("sum_z"):
         total = zsend[z_hi, pl.ds(pl.multiple_of(z_lo * 8, 8), 8)]
@@ -392,7 +416,9 @@
                 for step in range(2)
             ]
             beyond = lax.broadcasted_iota(jnp.int32, (24, 384), 0) == 16
-            state = [fields[j, 248:272, :] for j in range(5)]
+            state = [
+                jnp.concatenate([fields[j, 248:272, :], tail[j]], axis=1) for j in range(5)
+            ]
             rest = [jnp.where(beyond, 1.0, value) for value in state[3:5]]
             values = state[0:3]
             terms = face_terms(*rest)
@@ -456,7 +482,7 @@
         scratch_shapes=[
             pltpu.VMEM((16, 1024, 256), BF16),
             pltpu.VMEM((128, 128), F32),
-            pltpu.VMEM((512, 128), F32),
+            pltpu.VMEM((32, 128), F32),
             pltpu.VMEM((256, 256), jnp.int32),
             pltpu.VMEM((32, 128), jnp.int32),
             pltpu.VMEM((32, 1024), BF16),
@@ -471,9 +497,11 @@
             pltpu.VMEM((7, 8, 256), F32),
             pltpu.VMEM((8, 128), F32),
             pltpu.VMEM((512, 128), F32),
-            pltpu.VMEM((5, 272, 384), F32),
-            pltpu.VMEM((2, 16, 384), F32),
-            pltpu.VMEM((2, 16, 384), F32),
+            pltpu.VMEM((5, 272, 256), F32),
+            pltpu.VMEM((2, 24, 384), F32),
+            pltpu.VMEM((2, 24, 384), F32),
+            pltpu.VMEM((5, 16, 384), F32),
+            pltpu.VMEM((5, 24, 128), F32),
             pltpu.VMEM((128, 384), BF16),
             pltpu.VMEM((8, 384), F32),
             pltpu.VMEM((128, 256), BF16),

time: 32.1 us -> 30 us (0.935)
  Pallas kernels: 31.4 us -> 29.3 us
    pallas_call x1, Pallas kernels: 30.5 us -> 28.4 us  [on_device(): pl.pallas_call(kernel, out_shape=shapes, in_specs=[pl.BlockSpec(memory_sp...]
where the time goes in v4:
time: 30 us; the launch traced here: 29.9 us
  Pallas kernels  29.3 us (98%)
  between operations  0.64 us (2%)
    pallas_call x1, Pallas kernels, on_device(): pl.pallas_call(kernel, out_shape=shapes, in_specs=[pl.BlockSpec(memory_sp...  28.4 us
    pallas_call x1, Pallas kernels, on_device(): pl.pallas_call(write_out, out_shape=shapes, in_specs=[pl.BlockSpec(memory...  0.92 us

profile of v4, /device:TPU:1, one launch (start us, length us, event | category | flops | bytes accessed | tf_op | source)
XLA Modules:
  0.0 29.9 jit_solution(5889940363197923114)
XLA Ops:
  0.6 28.4 %shard_map.120 = (f32[8,256]{1,0:T(8,128)S(1)}, f32[256,256]{1,0:T(8,128)S(1)}, f32[256,256]{1,0:T(8,128)S(1)}, f32[256,256]{1,0:T(8,128)S(1)}) custom-call(bf16[1024,4096]{1,0:T(8,128)(2,1)} %bitcast.3, f32[32,128]{1,0:T(8,128)} %bitcast.4, f32[256,256]{1,0:T(8,128)} %speed.1, s32[256,256]{1,0:T(8,128)} %mask.1, s32[32,128]{1,0:T(8,128)} %bitcast.5, ...), custom_call_target="tpu_custom_call" | custom-call | tf_op jit(solution)/shard_map/pallas_call | solution.py:477
  29.0 0.9 %shard_map.121 = (f32[8,256]{1,0:T(8,128)}, f32[256,256]{1,0:T(8,128)}, f32[256,256]{1,0:T(8,128)}, f32[256,256]{1,0:T(8,128)}) custom-call(f32[8,256]{1,0:T(8,128)S(1)} %get-tuple-element.8.refs_0_, f32[256,256]{1,0:T(8,128)S(1)} %get-tuple-element.9.refs_1_, f32[256,256]{1,0:T(8,128)S(1)} %get-tuple-element.10.refs_2_, ...), custom_call_target="tpu_custom_call" | custom-call | tf_op jit(solution)/shard_map/pallas_call | solution.py:523

commit v5 on v4

--- a/solution.py
+++ b/solution.py
@@ -13,7 +13,7 @@
 HIGH = lax.Precision.HIGHEST
 MESH = pl.DeviceIdType.MESH
 ORDER = (2, 1, 3, 0)
-LOADS = (0, 1, 4, 5, 2, 3, 8, 9, 6, 7, 12, 13, 10, 11, 14, 15)
+LOADS = (0, 4, 8, 12, 1, 5, 9, 13, 2, 6, 10, 14, 3, 7, 11, 15)
 
 
 def transform_tables():
@@ -100,10 +100,23 @@
     west, east = (row, (col + 15) % 16), (row, (col + 1) % 16)
 
     with jax.named_scope("start_loads"):
-        local = [pltpu.make_async_copy(table.at[row], tab, lsem.at[0])]
-        local[0].start()
-        local.append(pltpu.make_async_copy(coef, cbuf, lsem.at[1]))
-        local[1].start()
+        local = [
+            pltpu.make_async_copy(coef, cbuf, lsem.at[1]),
+            pltpu.make_async_copy(table.at[row], tab, lsem.at[0]),
+        ]
+        for copy in local:
+            copy.start()
+        inner = (pl.ds(8, 256), slice(None))
+        grids = [
+            pltpu.make_async_copy(ref, fields.at[(j, *inner)], lsem.at[2 + j])
+            for j, ref in enumerate((surf, flow_x, flow_y, speed))
+        ]
+        grids += [
+            pltpu.make_async_copy(mask, mbuf, lsem.at[6]),
+            pltpu.make_async_copy(cells, cellbuf, lsem.at[7]),
+        ]
+        for copy in grids:
+            copy.start()
         loads = []
         for i, d in enumerate(ORDER):
             for side, par in enumerate((1 - core, core)):
@@ -117,24 +130,19 @@
                     )
         for slot in LOADS[0:4]:
             loads[slot].start()
-        inner = (pl.ds(8, 256), slice(None))
-        grids = [
-            pltpu.make_async_copy(ref, fields.at[(j, *inner)], lsem.at[2 + j])
-            for j, ref in enumerate((surf, flow_x, flow_y, speed))
-        ]
-        grids += [
-            pltpu.make_async_copy(mask, mbuf, lsem.at[6]),
-            pltpu.make_async_copy(cells, cellbuf, lsem.at[7]),
-        ]
-        for copy in grids:
-            copy.start()
-        for slot in LOADS[4:]:
-            loads[slot].start()
 
     with jax.named_scope("greet_peers"):
         barrier = pltpu.get_barrier_semaphore()
-        for peer in [partner, *y_peer[1:], *x_peer[1:], *z_peer[1:], north, south, west, east]:
+        for peer in [partner, *y_peer[1:], *x_peer[1:], *z_peer[1:]]:
             pl.semaphore_signal(barrier, inc=1, device_id=peer, device_id_type=MESH)
+        around = ((north, row > 0), (south, row < 15), (west, col > 0), (east, col < 15))
+        greetings = 14 + jnp.where(x == 3, 16 - is_edge.astype(jnp.int32), 0)
+        for peer, inside in around:
+            greetings = greetings + inside.astype(jnp.int32)
+
+            @pl.when(inside)
+            def _():
+                pl.semaphore_signal(barrier, inc=1, device_id=peer, device_id_type=MESH)
 
         @pl.when(is_edge)
         def _():
@@ -148,9 +156,16 @@
                     else:
                         greet()
 
+    with jax.named_scope("more_loads"):
+        for slot in LOADS[4:]:
+            loads[slot].start()
+
+    with jax.named_scope("wait_coef"):
+        local[0].wait()
+    with jax.named_scope("wait_table"):
+        local[1].wait()
+
     with jax.named_scope("build_left"):
-        for copy in local:
-            copy.wait()
         tables = tab[...]
         tiled = lax.dot_general(
             tables[32:96], jnp.concatenate([cbuf[...]] * 16, axis=0), (((1,), (1,)), ((), ())),
@@ -162,85 +177,144 @@
         left[:, 0:512] = jnp.where(diagonal, tiled[0:32], 0.0).astype(BF16)
         left[:, 512:1024] = jnp.where(diagonal, tiled[32:64], 0.0).astype(BF16)
 
-        dcopy, ycopy = [], {}
-
-        def part_of(i, side, target):
-            for part in range(2):
-                slot = i * 4 + side * 2 + part
-                loads[slot].wait()
-                target[i, :, part * 256 : part * 256 + 256] = jnp.dot(
-                    left[...], kbuf[slot], preferred_element_type=F32
+        dcopy, ycopy, xcopy = {}, {}, {}
+
+        def products(part, side, target):
+            for i in range(4):
+                loads[i * 4 + side * 2 + part].wait()
+            for i in range(4):
+                target[part, i] = jnp.dot(
+                    left[...], kbuf[i * 4 + side * 2 + part], preferred_element_type=F32
                 )
 
-        def other(i):
-            part_of(i, 0, dsend)
-            if i == 0:
-                pl.semaphore_wait(
-                    barrier, 18 + jnp.where(x == 3, 16 - is_edge.astype(jnp.int32), 0)
+        def to_partner(part):
+            dcopy[part] = pltpu.make_async_remote_copy(
+                src_ref=dsend.at[part], dst_ref=drecv.at[part],
+                send_sem=dsem.at[0, part], recv_sem=dsem.at[1, part],
+                device_id=partner, device_id_type=MESH,
+            )
+            dcopy[part].start()
+
+        def merge(part):
+            dcopy[part].wait_recv()
+            for i, d in enumerate(ORDER):
+                total = own[part, i] + drecv[part, i]
+                if d == 0:
+                    own[part, i] = total
+                    continue
+                ysend[part, d - 1] = total
+                ycopy[part, d] = pltpu.make_async_remote_copy(
+                    src_ref=ysend.at[part, d - 1], dst_ref=yrecv.at[part, d - 1],
+                    send_sem=ysem.at[0, part, d - 1], recv_sem=ysem.at[1, part, d - 1],
+                    device_id=y_peer[d], device_id_type=MESH,
                 )
-            copy = pltpu.make_async_remote_copy(
-                src_ref=dsend.at[i], dst_ref=drecv.at[i],
-                send_sem=dsem.at[0, i], recv_sem=dsem.at[1, i],
-                device_id=partner, device_id_type=MESH,
-            )
-            copy.start()
-            dcopy.append(copy)
-
-        def mine(i):
-            part_of(i, 1, own)
-
-        def merge(i):
-            d = ORDER[i]
-            dcopy[i].wait_recv()
-            total = own[i] + drecv[i]
-            if d == 0:
-                own[i] = total
-                return
-            ysend[d - 1] = total
-            ycopy[d] = pltpu.make_async_remote_copy(
-                src_ref=ysend.at[d - 1], dst_ref=yrecv.at[d - 1],
-                send_sem=ysem.at[0, d - 1], recv_sem=ysem.at[1, d - 1],
-                device_id=y_peer[d], device_id_type=MESH,
-            )
-            ycopy[d].start()
+                ycopy[part, d].start()
+
+        def sum_y(part):
+            total = own[part, 3]
+            for d in (1, 3, 2):
+                ycopy[part, d].wait_recv()
+                total = total + yrecv[part, d - 1]
+            split = split_rows(total)
+            stack = jnp.concatenate([split[k] for k in (0, 1, 0, 2, 0, 1)], axis=0)
+            partial = jnp.dot(wide[:, 0:192], stack, preferred_element_type=F32)
+            for at in range(4):
+                xsend[part, at] = partial[at * 32 : at * 32 + 32]
+            for d in (2, 1, 3):
+                xcopy[part, d] = pltpu.make_async_remote_copy(
+                    src_ref=xsend.at[part, (x + d) % 4], dst_ref=xrecv.at[part, d - 1],
+                    send_sem=xsem.at[0, part, d - 1], recv_sem=xsem.at[1, part, d - 1],
+                    device_id=x_peer[d], device_id_type=MESH,
+                )
+                xcopy[part, d].start()
+
+        def z_copy(part, k):
+            lo = (z_lo + k) % 4
+            d = (part * 4 + lo + 8 - z) % 8
+            at = (d + 7) % 8
+            return d, pltpu.make_async_remote_copy(
+                src_ref=zsend.at[part, pl.ds(pl.multiple_of(lo * 8, 8), 8)],
+                dst_ref=zrecv.at[at],
+                send_sem=zsem.at[0, at], recv_sem=zsem.at[1, at],
+                device_id=place(x, y, part * 4 + lo, core), device_id_type=MESH,
+            )
+
+        def sum_x(part):
+            total = xsend[part, x]
+            for d in (1, 3, 2):
+                xcopy[part, d].wait_recv()
+                total = total + xrecv[part, d - 1]
+            zsend[part] = total
+            for step in range(2):
+                for half in range(2):
+                    at = step * 4 + part * 2 + half
+                    gsend[at : at + 1] = total[30 + step : 31 + step, half * 128 : half * 128 + 128]
+            for k in (2, 1, 3, 0):
+                d, copy = z_copy(part, k)
+                if k == 0:
+                    pl.when(d != 0)(copy.start)
+                else:
+                    copy.start()
+
+        def strip(at, carry):
+            base = pl.multiple_of(at * 32, 8)
+            state = [fields[j, pl.ds(base, 48), :] for j in range(5)]
+            values, rest = state[0:3], state[3:5]
+            terms = face_terms(*rest)
+            for _ in range(2):
+                values = advance(*values, *rest, terms)
+            for ref, value in zip((surf_o, flow_x_o, flow_y_o), values):
+                ref[pl.ds(base, 32), :] = value[8:40]
+            return carry
 
     with jax.named_scope("spectrum"):
-        other(0)
-        other(1)
-
+        products(0, 0, dsend)
+    with jax.named_scope("barrier"):
+        pl.semaphore_wait(barrier, greetings)
+    with jax.named_scope("spectrum_1"):
+        to_partner(0)
+        products(1, 0, dsend)
+        to_partner(1)
+    with jax.named_scope("row_halos"):
         for copy in grids:
             copy.wait()
         fields[(4, *inner)] = mbuf[...].astype(F32)
         ns_copies = []
-        for at, (first, last, peer) in enumerate(((8, 264, north), (256, 0, south))):
+        for at, (first, last, peer, inside) in enumerate(
+            ((8, 264, north, row > 0), (256, 0, south, row < 15))
+        ):
             copy = pltpu.make_async_remote_copy(
                 src_ref=fields.at[:, pl.ds(first, 8)],
                 dst_ref=fields.at[:, pl.ds(last, 8)],
                 send_sem=nssem.at[0, at], recv_sem=nssem.at[1, at],
                 device_id=peer, device_id_type=MESH,
             )
-            copy.start()
-            ns_copies.append(copy)
-        mine(0)
-        other(2)
-        mine(1)
+            pl.when(inside)(copy.start)
+            ns_copies.append((copy, inside))
+    with jax.named_scope("spectrum_2"):
+        products(0, 1, own)
+    with jax.named_scope("merge_0"):
         merge(0)
-        other(3)
-        mine(2)
+    with jax.named_scope("spectrum_3"):
+        products(1, 1, own)
+    with jax.named_scope("merge_1"):
         merge(1)
-        mine(3)
-        merge(2)
 
     with jax.named_scope("widen"):
         split = split_rows(tables[0:32])
         wide[...] = jnp.concatenate(
             [*(split[k].astype(F32) for k in (0, 0, 1, 0, 2, 1)), jnp.zeros((64, 128), F32)], axis=0
         ).T.astype(BF16)
-        merge(3)
+    with jax.named_scope("water"):
+        lax.fori_loop(1, 5, strip, 0)
+    with jax.named_scope("sum_y_0"):
+        sum_y(0)
+    with jax.named_scope("sum_y_1"):
+        sum_y(1)
 
     with jax.named_scope("column_halos"):
-        for copy in ns_copies:
-            copy.wait_recv()
+        pl.when(row < 15)(ns_copies[0][0].wait_recv)
+        pl.when(row > 0)(ns_copies[1][0].wait_recv)
 
         @pl.when(row == 0)
         def _():
@@ -252,7 +326,9 @@
 
         lane = lax.broadcasted_iota(jnp.int32, (272, 128), 1)
         ew_copies = []
-        for at, (first, shift, peer) in enumerate(((0, 0, west), (128, 4, east))):
+        for at, (first, shift, peer, inside) in enumerate(
+            ((0, 0, west, col > 0), (128, 4, east, col < 15))
+        ):
             packed = jnp.zeros((272, 128), F32)
             for j in range(5):
                 block = fields[j, :, first : first + 128]
@@ -266,27 +342,33 @@
                 send_sem=ewsem.at[0, at], recv_sem=ewsem.at[1, at],
                 device_id=peer, device_id_type=MESH,
             )
-            copy.start()
-            ew_copies.append(copy)
-
-    with jax.named_scope("sum_y"):
-        total = own[3]
-        for d in (1, 3, 2):
-            ycopy[d].wait_recv()
-            total = total + yrecv[d - 1]
-        split = split_rows(total)
-        stack = jnp.concatenate([split[k] for k in (0, 1, 0, 2, 0, 1)], axis=0)
-        partial = jnp.dot(wide[:, 0:192], stack, preferred_element_type=F32)
-        for at in range(4):
-            xsend[at] = partial[at * 32 : at * 32 + 32]
-        xcopy = {}
-        for d in (2, 1, 3):
-            xcopy[d] = pltpu.make_async_remote_copy(
-                src_ref=xsend.at[(x + d) % 4], dst_ref=xrecv.at[d - 1],
-                send_sem=xsem.at[0, d - 1], recv_sem=xsem.at[1, d - 1],
-                device_id=x_peer[d], device_id_type=MESH,
-            )
-            xcopy[d].start()
+            pl.when(inside)(copy.start)
+            ew_copies.append((copy, inside))
+
+    with jax.named_scope("water_1"):
+        lax.fori_loop(5, 7, strip, 0)
+    with jax.named_scope("sum_x_0"):
+        sum_x(0)
+    with jax.named_scope("sum_x_1"):
+        sum_x(1)
+
+    with jax.named_scope("ghost_send"):
+        here = pl.ds(pl.multiple_of((z * 8 + y * 2 + core) * 8, 8), 8)
+
+        def ghost_copy(index):
+            return pltpu.make_async_remote_copy(
+                src_ref=gsend, dst_ref=grecv.at[here],
+                send_sem=gssem.at[index], recv_sem=grsem,
+                device_id=(15, index), device_id_type=MESH,
+            )
+
+        @pl.when(x == 3)
+        def _():
+            for index in range(16):
+                pl.when((row != 15) | (col != index))(ghost_copy(index).start)
+
+    with jax.named_scope("more_water"):
+        lax.fori_loop(0, 2, lambda at, carry: strip(at * 7, carry), 0)
 
     with jax.named_scope("selection"):
         @pl.when(is_edge)
@@ -302,59 +384,15 @@
             onehot[...] = jnp.where(found > 0.0, 1.0, 0.0).astype(BF16)
             blocks[...] = jnp.broadcast_to(jnp.sum(found, axis=0, keepdims=True), (8, 384))
 
-    with jax.named_scope("water"):
-        def strip(at, carry):
-            base = pl.multiple_of(at * 32, 8)
-            state = [fields[j, pl.ds(base, 48), :] for j in range(5)]
-            values, rest = state[0:3], state[3:5]
-            terms = face_terms(*rest)
-            for _ in range(2):
-                values = advance(*values, *rest, terms)
-            for ref, value in zip((surf_o, flow_x_o, flow_y_o), values):
-                ref[pl.ds(base, 32), :] = value[8:40]
-            return carry
-
-        lax.fori_loop(0, 8, strip, 0)
-
-    with jax.named_scope("sum_x"):
-        total = xsend[x]
-        for d in (1, 3, 2):
-            xcopy[d].wait_recv()
-            total = total + xrecv[d - 1]
-        zsend[0] = total[:, 0:256]
-        zsend[1] = total[:, 256:512]
-        for at in range(8):
-            gsend[at : at + 1] = total[30 + at // 4 : 31 + at // 4, at % 4 * 128 : at % 4 * 128 + 128]
-        here = pl.ds(pl.multiple_of((z * 8 + y * 2 + core) * 8, 8), 8)
-
-        def ghost_copy(index):
-            return pltpu.make_async_remote_copy(
-                src_ref=gsend, dst_ref=grecv.at[here],
-                send_sem=gssem.at[index], recv_sem=grsem,
-                device_id=(15, index), device_id_type=MESH,
-            )
-
-        @pl.when(x == 3)
-        def _():
-            for index in range(16):
-                pl.when((row != 15) | (col != index))(ghost_copy(index).start)
-
-        zcopy = {}
-        for d in (4, 3, 5, 2, 6, 1, 7):
-            to = (z + d) % 8
-            zcopy[d] = pltpu.make_async_remote_copy(
-                src_ref=zsend.at[to // 4, pl.ds(pl.multiple_of((to % 4) * 8, 8), 8)],
-                dst_ref=zrecv.at[d - 1],
-                send_sem=zsem.at[0, d - 1], recv_sem=zsem.at[1, d - 1],
-                device_id=z_peer[d], device_id_type=MESH,
-            )
-            zcopy[d].start()
-
     with jax.named_scope("side_water"):
-        for copy in ew_copies:
-            copy.wait_recv()
-        from_east = jnp.where(col == 15, 0.0, ewrecv[0])
-        from_west = jnp.where(col == 0, 0.0, ewrecv[1])
+        for at, ((copy, _), inside) in enumerate(zip(ew_copies, (col < 15, col > 0))):
+            pl.when(inside)(copy.wait_recv)
+
+            @pl.when(~inside)
+            def _():
+                ewrecv[at] = jnp.zeros((24, 384), F32)
+
+        from_east, from_west = ewrecv[0], ewrecv[1]
         for j in range(5):
             for at, piece in enumerate((from_west, ewsend[0], ewsend[1], from_east)):
                 sides[j, at * 4 : at * 4 + 4] = piece[j * 4 : j * 4 + 4]
@@ -389,7 +427,7 @@
     with jax.named_scope("sum_z"):
         total = zsend[z_hi, pl.ds(pl.multiple_of(z_lo * 8, 8), 8)]
         for d in range(1, 8):
-            zcopy[d].wait_recv()
+            pltpu.make_async_copy(zrecv.at[d - 1], zrecv.at[d - 1], zsem.at[1, d - 1]).wait()
             total = total + zrecv[d - 1]
         series_o[...] = total
 
@@ -433,8 +471,14 @@
                 ref[248:256, :] = value[8:16, 0:256]
 
     with jax.named_scope("drain"):
-        for copy in [*dcopy, *ycopy.values(), *xcopy.values(), *zcopy.values(), *ns_copies, *ew_copies]:
+        for copy in [*dcopy.values(), *ycopy.values(), *xcopy.values()]:
             copy.wait_send()
+        for copy, inside in [*ns_copies, *ew_copies]:
+            pl.when(inside)(copy.wait_send)
+        for part in range(2):
+            for k in range(4):
+                d, copy = z_copy(part, k)
+                pl.when(d != 0)(copy.wait_send)
 
         @pl.when(x == 3)
         def _():
@@ -486,13 +530,13 @@
             pltpu.VMEM((256, 256), jnp.int32),
             pltpu.VMEM((32, 128), jnp.int32),
             pltpu.VMEM((32, 1024), BF16),
-            pltpu.VMEM((4, 32, 512), F32),
-            pltpu.VMEM((4, 32, 512), F32),
-            pltpu.VMEM((4, 32, 512), F32),
-            pltpu.VMEM((3, 32, 512), F32),
-            pltpu.VMEM((3, 32, 512), F32),
-            pltpu.VMEM((4, 32, 512), F32),
-            pltpu.VMEM((3, 32, 512), F32),
+            pltpu.VMEM((2, 4, 32, 256), F32),
+            pltpu.VMEM((2, 4, 32, 256), F32),
+            pltpu.VMEM((2, 4, 32, 256), F32),
+            pltpu.VMEM((2, 3, 32, 256), F32),
+            pltpu.VMEM((2, 3, 32, 256), F32),
+            pltpu.VMEM((2, 4, 32, 256), F32),
+            pltpu.VMEM((2, 3, 32, 256), F32),
             pltpu.VMEM((2, 32, 256), F32),
             pltpu.VMEM((7, 8, 256), F32),
             pltpu.VMEM((8, 128), F32),
@@ -507,10 +551,10 @@
             pltpu.VMEM((128, 256), BF16),
             dma((16,)),
             dma((8,)),
-            dma((2, 4)),
-            dma((2, 3)),
-            dma((2, 3)),
-            dma((2, 7)),
+            dma((2, 2)),
+            dma((2, 2, 3)),
+            dma((2, 2, 3)),
+            dma((2, 8)),
             dma((16,)),
             dma(()),
             dma((2, 2)),

time: 30 us -> 26.9 us (0.90)
  the two profiles are of different devices: /device:TPU:1 before, /device:TPU:2 now
where the time goes in v5:
time: 26.9 us; the launch traced here: 26.7 us
  Pallas kernels  26.1 us (97%)
  between operations  0.64 us (2%)
    pallas_call x1, Pallas kernels, on_device(): pl.pallas_call(kernel, out_shape=shapes, in_specs=[pl.BlockSpec(memory_sp...  25.2 us
    pallas_call x1, Pallas kernels, on_device(): pl.pallas_call(write_out, out_shape=shapes, in_specs=[pl.BlockSpec(memory...  0.92 us

profile of v5, /device:TPU:2, one launch (start us, length us, event | category | flops | bytes accessed | tf_op | source)
XLA Modules:
  0.0 26.7 jit_solution(7263129723987896201)
XLA Ops:
  0.6 25.2 %shard_map.120 = (f32[8,256]{1,0:T(8,128)S(1)}, f32[256,256]{1,0:T(8,128)S(1)}, f32[256,256]{1,0:T(8,128)S(1)}, f32[256,256]{1,0:T(8,128)S(1)}) custom-call(bf16[1024,4096]{1,0:T(8,128)(2,1)} %bitcast.3, f32[32,128]{1,0:T(8,128)} %bitcast.4, f32[256,256]{1,0:T(8,128)} %speed.1, s32[256,256]{1,0:T(8,128)} %mask.1, s32[32,128]{1,0:T(8,128)} %bitcast.5, ...), custom_call_target="tpu_custom_call" | custom-call | tf_op jit(solution)/shard_map/pallas_call | solution.py:521
  25.8 0.9 %shard_map.121 = (f32[8,256]{1,0:T(8,128)}, f32[256,256]{1,0:T(8,128)}, f32[256,256]{1,0:T(8,128)}, f32[256,256]{1,0:T(8,128)}) custom-call(f32[8,256]{1,0:T(8,128)S(1)} %get-tuple-element.8.refs_0_, f32[256,256]{1,0:T(8,128)S(1)} %get-tuple-element.9.refs_1_, f32[256,256]{1,0:T(8,128)S(1)} %get-tuple-element.10.refs_2_, ...), custom_call_target="tpu_custom_call" | custom-call | tf_op jit(solution)/shard_map/pallas_call | solution.py:567

commit v6 on v5

--- a/solution.py
+++ b/solution.py
@@ -80,8 +80,8 @@
     kern, coef, speed, mask, cells, surf, flow_x, flow_y, table,
     series_o, surf_o, flow_x_o, flow_y_o,
     kbuf, tab, cbuf, mbuf, cellbuf, left, own, dsend, drecv, ysend, yrecv,
-    xsend, xrecv, zsend, zrecv, gsend, grecv, fields, ewsend, ewrecv, sides, tail, onehot, blocks, wide,
-    ksem, lsem, dsem, ysem, xsem, zsem, gssem, grsem, nssem, ewsem,
+    xsend, xrecv, zsend, zrecv, gsend, gearly, gtotal, gpair, grecv, fields, ewsend, ewrecv, sides, tail, onehot, blocks, wide,
+    ksem, lsem, dsem, ysem, xsem, zsem, gxsem, gpsem, gssem, grsem, nssem, ewsem, known,
 ):
     row, col = lax.axis_index("rows"), lax.axis_index("cols")
     x, z_lo = row % 4, row // 4
@@ -105,17 +105,6 @@
             pltpu.make_async_copy(table.at[row], tab, lsem.at[0]),
         ]
         for copy in local:
-            copy.start()
-        inner = (pl.ds(8, 256), slice(None))
-        grids = [
-            pltpu.make_async_copy(ref, fields.at[(j, *inner)], lsem.at[2 + j])
-            for j, ref in enumerate((surf, flow_x, flow_y, speed))
-        ]
-        grids += [
-            pltpu.make_async_copy(mask, mbuf, lsem.at[6]),
-            pltpu.make_async_copy(cells, cellbuf, lsem.at[7]),
-        ]
-        for copy in grids:
             copy.start()
         loads = []
         for i, d in enumerate(ORDER):
@@ -133,35 +122,36 @@
 
     with jax.named_scope("greet_peers"):
         barrier = pltpu.get_barrier_semaphore()
-        for peer in [partner, *y_peer[1:], *x_peer[1:], *z_peer[1:]]:
+        near = [partner, *y_peer[1:], *x_peer[1:], *(z_peer[d] for d in (1, 2, 6, 7))]
+        for peer in near:
             pl.semaphore_signal(barrier, inc=1, device_id=peer, device_id_type=MESH)
-        around = ((north, row > 0), (south, row < 15), (west, col > 0), (east, col < 15))
-        greetings = 14 + jnp.where(x == 3, 16 - is_edge.astype(jnp.int32), 0)
-        for peer, inside in around:
+        greetings = len(near)
+        for peer, inside in ((north, row > 0), (south, row < 15)):
             greetings = greetings + inside.astype(jnp.int32)
 
             @pl.when(inside)
             def _():
                 pl.semaphore_signal(barrier, inc=1, device_id=peer, device_id_type=MESH)
 
-        @pl.when(is_edge)
-        def _():
-            for at_row in (3, 7, 11, 15):
-                for at_col in range(16):
-                    def greet(peer=(at_row, at_col)):
-                        pl.semaphore_signal(barrier, inc=1, device_id=peer, device_id_type=MESH)
-
-                    if at_row == 15:
-                        pl.when(col != at_col)(greet)
-                    else:
-                        greet()
-
     with jax.named_scope("more_loads"):
-        for slot in LOADS[4:]:
+        for slot in LOADS[4:8]:
             loads[slot].start()
+        inner = (pl.ds(8, 256), slice(None))
+        grids = [
+            pltpu.make_async_copy(ref, fields.at[(j, *inner)], lsem.at[2 + j])
+            for j, ref in enumerate((surf, flow_x, flow_y, speed))
+        ]
+        grids += [
+            pltpu.make_async_copy(mask, mbuf, lsem.at[6]),
+            pltpu.make_async_copy(cells, cellbuf, lsem.at[7]),
+        ]
+        for copy in grids:
+            copy.start()
 
     with jax.named_scope("wait_coef"):
         local[0].wait()
+        for slot in LOADS[8:]:
+            loads[slot].start()
     with jax.named_scope("wait_table"):
         local[1].wait()
 
@@ -210,6 +200,22 @@
                 )
                 ycopy[part, d].start()
 
+        def early_ghost(d):
+            return pltpu.make_async_remote_copy(
+                src_ref=gsend, dst_ref=gearly.at[d],
+                send_sem=gxsem.at[0], recv_sem=gxsem.at[1 + d],
+                device_id=place(3, y, z, core), device_id_type=MESH,
+            )
+
+        def ahead(part, partial):
+            for step in range(2):
+                for half in range(2):
+                    at = step * 4 + part * 2 + half
+                    line = 126 + step
+                    gsend[at : at + 1] = partial[line : line + 1, half * 128 : half * 128 + 128]
+            if part == 1:
+                pl.when(x < 3)(early_ghost(x).start)
+
         def sum_y(part):
             total = own[part, 3]
             for d in (1, 3, 2):
@@ -220,6 +226,7 @@
             partial = jnp.dot(wide[:, 0:192], stack, preferred_element_type=F32)
             for at in range(4):
                 xsend[part, at] = partial[at * 32 : at * 32 + 32]
+            ahead(part, partial)
             for d in (2, 1, 3):
                 xcopy[part, d] = pltpu.make_async_remote_copy(
                     src_ref=xsend.at[part, (x + d) % 4], dst_ref=xrecv.at[part, d - 1],
@@ -245,10 +252,6 @@
                 xcopy[part, d].wait_recv()
                 total = total + xrecv[part, d - 1]
             zsend[part] = total
-            for step in range(2):
-                for half in range(2):
-                    at = step * 4 + part * 2 + half
-                    gsend[at : at + 1] = total[30 + step : 31 + step, half * 128 : half * 128 + 128]
             for k in (2, 1, 3, 0):
                 d, copy = z_copy(part, k)
                 if k == 0:
@@ -306,9 +309,11 @@
             [*(split[k].astype(F32) for k in (0, 0, 1, 0, 2, 1)), jnp.zeros((64, 128), F32)], axis=0
         ).T.astype(BF16)
     with jax.named_scope("water"):
-        lax.fori_loop(1, 5, strip, 0)
+        lax.fori_loop(1, 3, strip, 0)
     with jax.named_scope("sum_y_0"):
         sum_y(0)
+        for at, d in enumerate((2, 6)):
+            pl.semaphore_signal(known.at[at], inc=1, device_id=z_peer[d], device_id_type=MESH)
     with jax.named_scope("sum_y_1"):
         sum_y(1)
 
@@ -342,33 +347,43 @@
                 send_sem=ewsem.at[0, at], recv_sem=ewsem.at[1, at],
                 device_id=peer, device_id_type=MESH,
             )
+            ew_copies.append((copy, inside))
+
+    with jax.named_scope("far"):
+        for at in range(2):
+            pl.semaphore_wait(known.at[at], 1)
+        for copy, inside in ew_copies:
             pl.when(inside)(copy.start)
-            ew_copies.append((copy, inside))
 
     with jax.named_scope("water_1"):
-        lax.fori_loop(5, 7, strip, 0)
+        lax.fori_loop(3, 6, strip, 0)
     with jax.named_scope("sum_x_0"):
         sum_x(0)
+    with jax.named_scope("ghost_send"):
+        here = pl.ds(pl.multiple_of((z * 4 + y) * 8, 8), 8)
+
+        def ghost_copy(index):
+            return pltpu.make_async_remote_copy(
+                src_ref=gtotal, dst_ref=grecv.at[here],
+                send_sem=gssem.at[index], recv_sem=grsem,
+                device_id=(15, index * 2 + core), device_id_type=MESH,
+            )
+
+        @pl.when(x == 3)
+        def _():
+            total = gsend[...]
+            for d in range(3):
+                early_ghost(d).wait_recv()
+                total = total + gearly[d]
+            gtotal[...] = total
+            for index in range(8):
+                pl.when((row != 15) | (col != index * 2 + core))(ghost_copy(index).start)
+
     with jax.named_scope("sum_x_1"):
         sum_x(1)
 
-    with jax.named_scope("ghost_send"):
-        here = pl.ds(pl.multiple_of((z * 8 + y * 2 + core) * 8, 8), 8)
-
-        def ghost_copy(index):
-            return pltpu.make_async_remote_copy(
-                src_ref=gsend, dst_ref=grecv.at[here],
-                send_sem=gssem.at[index], recv_sem=grsem,
-                device_id=(15, index), device_id_type=MESH,
-            )
-
-        @pl.when(x == 3)
-        def _():
-            for index in range(16):
-                pl.when((row != 15) | (col != index))(ghost_copy(index).start)
-
     with jax.named_scope("more_water"):
-        lax.fori_loop(0, 2, lambda at, carry: strip(at * 7, carry), 0)
+        lax.fori_loop(6, 9, lambda at, carry: strip(at % 8, carry), 0)
 
     with jax.named_scope("selection"):
         @pl.when(is_edge)
@@ -434,20 +449,30 @@
     with jax.named_scope("ghost"):
         @pl.when(is_edge)
         def _():
-            grecv[here] = gsend[...]
+            grecv[here] = gtotal[...]
             pltpu.make_async_copy(
-                grecv.at[pl.ds(0, 504)], grecv.at[pl.ds(0, 504)], grsem
+                grecv.at[pl.ds(0, 248)], grecv.at[pl.ds(0, 248)], grsem
             ).wait()
-            value = grecv[0:64]
+            value = grecv[0:32]
             for other_z in range(1, 8):
-                value = value + grecv[other_z * 64 : other_z * 64 + 64]
+                value = value + grecv[other_z * 32 : other_z * 32 + 32]
+            gpair[core] = value
+            share = pltpu.make_async_remote_copy(
+                src_ref=gpair.at[core], dst_ref=gpair.at[core],
+                send_sem=gpsem.at[0], recv_sem=gpsem.at[1],
+                device_id=partner, device_id_type=MESH,
+            )
+            share.start()
+            share.wait_send()
+            share.wait_recv()
+            value = jnp.concatenate([gpair[0], gpair[1]], axis=0)
             picked = jnp.dot(
                 jnp.concatenate(split_rows(value), axis=0), onehot[...],
                 preferred_element_type=F32,
             )
             picked = picked[128:192] + picked[64:128] + picked[0:64]
             at = lax.broadcasted_iota(jnp.int32, (64, 384), 0)
-            block = (at >> 4) * 8 + (at & 2) * 2 + ((at >> 3) & 1) * 2 + (at & 1)
+            block = ((at >> 3) & 3) * 8 + (at & 2) * 2 + (at >> 5) * 2 + (at & 1)
             picked = jnp.where((block + 1).astype(F32) == blocks[0:1], picked, 0.0)
             ghost = [
                 jnp.sum(jnp.where(((at >> 2) & 1) == step, picked, 0.0), axis=0, keepdims=True)
@@ -479,11 +504,12 @@
             for k in range(4):
                 d, copy = z_copy(part, k)
                 pl.when(d != 0)(copy.wait_send)
+        pl.when(x < 3)(early_ghost(x).wait_send)
 
         @pl.when(x == 3)
         def _():
-            for index in range(16):
-                pl.when((row != 15) | (col != index))(ghost_copy(index).wait_send)
+            for index in range(8):
+                pl.when((row != 15) | (col != index * 2 + core))(ghost_copy(index).wait_send)
 
 
 def write_out(*refs):
@@ -540,7 +566,10 @@
             pltpu.VMEM((2, 32, 256), F32),
             pltpu.VMEM((7, 8, 256), F32),
             pltpu.VMEM((8, 128), F32),
-            pltpu.VMEM((512, 128), F32),
+            pltpu.VMEM((3, 8, 128), F32),
+            pltpu.VMEM((8, 128), F32),
+            pltpu.VMEM((2, 32, 128), F32),
+            pltpu.VMEM((256, 128), F32),
             pltpu.VMEM((5, 272, 256), F32),
             pltpu.VMEM((2, 24, 384), F32),
             pltpu.VMEM((2, 24, 384), F32),
@@ -555,10 +584,13 @@
             dma((2, 2, 3)),
             dma((2, 2, 3)),
             dma((2, 8)),
-            dma((16,)),
+            dma((4,)),
+            dma((2,)),
+            dma((8,)),
             dma(()),
             dma((2, 2)),
             dma((2, 2)),
+            pltpu.SemaphoreType.REGULAR((2,)),
         ],
         compiler_params=pltpu.CompilerParams(
             collective_id=0, has_side_effects=True, vmem_limit_bytes=48 * 1024 * 1024

time: 26.9 us -> 26.2 us (0.974)
  the two profiles are of different devices: /device:TPU:2 before, /device:TPU:1 now
where the time goes in v6:
time: 26.2 us; the launch traced here: 26.1 us
  Pallas kernels  25.4 us (97%)
  between operations  0.64 us (2%)
    pallas_call x1, Pallas kernels, on_device(): pl.pallas_call(kernel, out_shape=shapes, in_specs=[pl.BlockSpec(memory_sp...  24.5 us
    pallas_call x1, Pallas kernels, on_device(): pl.pallas_call(write_out, out_shape=shapes, in_specs=[pl.BlockSpec(memory...  0.92 us

profile of v6, /device:TPU:1, one launch (start us, length us, event | category | flops | bytes accessed | tf_op | source)
XLA Modules:
  0.0 26.1 jit_solution(17473100889296825217)
XLA Ops:
  0.6 24.5 %shard_map.120 = (f32[8,256]{1,0:T(8,128)S(1)}, f32[256,256]{1,0:T(8,128)S(1)}, f32[256,256]{1,0:T(8,128)S(1)}, f32[256,256]{1,0:T(8,128)S(1)}) custom-call(bf16[1024,4096]{1,0:T(8,128)(2,1)} %bitcast.3, f32[32,128]{1,0:T(8,128)} %bitcast.4, f32[256,256]{1,0:T(8,128)} %speed.1, s32[256,256]{1,0:T(8,128)} %mask.1, s32[32,128]{1,0:T(8,128)} %bitcast.5, ...), custom_call_target="tpu_custom_call" | custom-call | tf_op jit(solution)/shard_map/pallas_call | solution.py:547
  25.2 0.9 %shard_map.121 = (f32[8,256]{1,0:T(8,128)}, f32[256,256]{1,0:T(8,128)}, f32[256,256]{1,0:T(8,128)}, f32[256,256]{1,0:T(8,128)}) custom-call(f32[8,256]{1,0:T(8,128)S(1)} %get-tuple-element.8.refs_0_, f32[256,256]{1,0:T(8,128)S(1)} %get-tuple-element.9.refs_1_, f32[256,256]{1,0:T(8,128)S(1)} %get-tuple-element.10.refs_2_, ...), custom_call_target="tpu_custom_call" | custom-call | tf_op jit(solution)/shard_map/pallas_call | solution.py:599

commit v7 on v6

--- a/solution.py
+++ b/solution.py
@@ -81,7 +81,7 @@
     series_o, surf_o, flow_x_o, flow_y_o,
     kbuf, tab, cbuf, mbuf, cellbuf, left, own, dsend, drecv, ysend, yrecv,
     xsend, xrecv, zsend, zrecv, gsend, gearly, gtotal, gpair, grecv, fields, ewsend, ewrecv, sides, tail, onehot, blocks, wide,
-    ksem, lsem, dsem, ysem, xsem, zsem, gxsem, gpsem, gssem, grsem, nssem, ewsem, known,
+    ksem, lsem, bsem, dsem, ysem, xsem, zsem, gxsem, gpsem, gssem, grsem, nssem, ewsem, known,
 ):
     row, col = lax.axis_index("rows"), lax.axis_index("cols")
     x, z_lo = row % 4, row // 4
@@ -101,10 +101,13 @@
 
     with jax.named_scope("start_loads"):
         local = [
+            pltpu.make_async_copy(
+                table.at[row, pl.ds(32, 64)], tab.at[pl.ds(32, 64)], lsem.at[0]
+            ),
             pltpu.make_async_copy(coef, cbuf, lsem.at[1]),
-            pltpu.make_async_copy(table.at[row], tab, lsem.at[0]),
+            pltpu.make_async_copy(table.at[row, pl.ds(0, 32)], tab.at[pl.ds(0, 32)], lsem.at[8]),
         ]
-        for copy in local:
+        for copy in local[0:2]:
             copy.start()
         loads = []
         for i, d in enumerate(ORDER):
@@ -136,29 +139,44 @@
     with jax.named_scope("more_loads"):
         for slot in LOADS[4:8]:
             loads[slot].start()
-        inner = (pl.ds(8, 256), slice(None))
+        sources = (surf, flow_x, flow_y, speed)
+        borders = []
+        for side, (source, target) in enumerate(((0, 8), (248, 256))):
+            for j in range(5):
+                at = bsem.at[side * 5 + j]
+                if j < 4:
+                    copy = pltpu.make_async_copy(
+                        sources[j].at[pl.ds(source, 8)], fields.at[j, pl.ds(target, 8)], at
+                    )
+                else:
+                    copy = pltpu.make_async_copy(
+                        mask.at[pl.ds(source, 8)], mbuf.at[pl.ds(source, 8)], at
+                    )
+                borders.append(copy)
+        for copy in borders:
+            copy.start()
+        middle = pl.ds(8, 240)
         grids = [
-            pltpu.make_async_copy(ref, fields.at[(j, *inner)], lsem.at[2 + j])
-            for j, ref in enumerate((surf, flow_x, flow_y, speed))
+            pltpu.make_async_copy(ref.at[middle], fields.at[j, pl.ds(16, 240)], lsem.at[2 + j])
+            for j, ref in enumerate(sources)
         ]
         grids += [
-            pltpu.make_async_copy(mask, mbuf, lsem.at[6]),
+            pltpu.make_async_copy(mask.at[middle], mbuf.at[middle], lsem.at[6]),
             pltpu.make_async_copy(cells, cellbuf, lsem.at[7]),
         ]
-        for copy in grids:
-            copy.start()
 
     with jax.named_scope("wait_coef"):
-        local[0].wait()
         for slot in LOADS[8:]:
             loads[slot].start()
+        for copy in [*grids, local[2]]:
+            copy.start()
+        local[0].wait()
     with jax.named_scope("wait_table"):
         local[1].wait()
 
     with jax.named_scope("build_left"):
-        tables = tab[...]
         tiled = lax.dot_general(
-            tables[32:96], jnp.concatenate([cbuf[...]] * 16, axis=0), (((1,), (1,)), ((), ())),
+            tab[32:96], jnp.concatenate([cbuf[...]] * 16, axis=0), (((1,), (1,)), ((), ())),
             precision=HIGH, preferred_element_type=F32,
         )
         lanes = lax.broadcasted_iota(jnp.int32, (32, 512), 1)
@@ -279,9 +297,10 @@
         products(1, 0, dsend)
         to_partner(1)
     with jax.named_scope("row_halos"):
-        for copy in grids:
+        for copy in borders:
             copy.wait()
-        fields[(4, *inner)] = mbuf[...].astype(F32)
+        for source in (0, 248):
+            fields[4, source + 8 : source + 16, :] = mbuf[source : source + 8].astype(F32)
         ns_copies = []
         for at, (first, last, peer, inside) in enumerate(
             ((8, 264, north, row > 0), (256, 0, south, row < 15))
@@ -298,22 +317,34 @@
         products(0, 1, own)
     with jax.named_scope("merge_0"):
         merge(0)
+        for d in range(1, 4):
+            pl.semaphore_signal(known.at[d + 1], inc=1, device_id=y_peer[d], device_id_type=MESH)
     with jax.named_scope("spectrum_3"):
         products(1, 1, own)
     with jax.named_scope("merge_1"):
         merge(1)
 
     with jax.named_scope("widen"):
-        split = split_rows(tables[0:32])
+        local[2].wait()
+        split = split_rows(tab[0:32])
         wide[...] = jnp.concatenate(
             [*(split[k].astype(F32) for k in (0, 0, 1, 0, 2, 1)), jnp.zeros((64, 128), F32)], axis=0
         ).T.astype(BF16)
+        for copy in grids:
+            copy.wait()
+        fields[4, 16:256, :] = mbuf[8:248].astype(F32)
+
     with jax.named_scope("water"):
         lax.fori_loop(1, 3, strip, 0)
+    with jax.named_scope("relay"):
+        for d in range(1, 4):
+            pl.semaphore_wait(known.at[d + 1], 1)
+        for at, d in enumerate((2, 6)):
+            pl.semaphore_signal(known.at[at], inc=1, device_id=z_peer[d], device_id_type=MESH)
+
     with jax.named_scope("sum_y_0"):
         sum_y(0)
-        for at, d in enumerate((2, 6)):
-            pl.semaphore_signal(known.at[at], inc=1, device_id=z_peer[d], device_id_type=MESH)
+
     with jax.named_scope("sum_y_1"):
         sum_y(1)
 
@@ -579,7 +610,8 @@
             pltpu.VMEM((8, 384), F32),
             pltpu.VMEM((128, 256), BF16),
             dma((16,)),
-            dma((8,)),
+            dma((9,)),
+            dma((10,)),
             dma((2, 2)),
             dma((2, 2, 3)),
             dma((2, 2, 3)),
@@ -590,7 +622,7 @@
             dma(()),
             dma((2, 2)),
             dma((2, 2)),
-            pltpu.SemaphoreType.REGULAR((2,)),
+            pltpu.SemaphoreType.REGULAR((5,)),
         ],
         compiler_params=pltpu.CompilerParams(
             collective_id=0, has_side_effects=True, vmem_limit_bytes=48 * 1024 * 1024

time: 26.2 us -> 25.9 us (0.989)
  Pallas kernels: 25.4 us -> 25 us
    pallas_call x1, Pallas kernels: 24.5 us -> 24.1 us  [on_device(): pl.pallas_call(kernel, out_shape=shapes, in_specs=[pl.BlockSpec(memory_sp...]
where the time goes in v7:
time: 25.9 us; the launch traced here: 25.6 us
  Pallas kernels  25 us (97%)
  between operations  0.64 us (2%)
    pallas_call x1, Pallas kernels, on_device(): pl.pallas_call(kernel, out_shape=shapes, in_specs=[pl.BlockSpec(memory_sp...  24.1 us
    pallas_call x1, Pallas kernels, on_device(): pl.pallas_call(write_out, out_shape=shapes, in_specs=[pl.BlockSpec(memory...  0.92 us

profile of v7, /device:TPU:1, one launch (start us, length us, event | category | flops | bytes accessed | tf_op | source)
XLA Modules:
  0.0 25.6 jit_solution(10105474111586107822)
XLA Ops:
  0.6 24.1 %shard_map.120 = (f32[8,256]{1,0:T(8,128)S(1)}, f32[256,256]{1,0:T(8,128)S(1)}, f32[256,256]{1,0:T(8,128)S(1)}, f32[256,256]{1,0:T(8,128)S(1)}) custom-call(bf16[1024,4096]{1,0:T(8,128)(2,1)} %bitcast.3, f32[32,128]{1,0:T(8,128)} %bitcast.4, f32[256,256]{1,0:T(8,128)} %speed.1, s32[256,256]{1,0:T(8,128)} %mask.1, s32[32,128]{1,0:T(8,128)} %bitcast.5, ...), custom_call_target="tpu_custom_call" | custom-call | tf_op jit(solution)/shard_map/pallas_call | solution.py:578
  24.7 0.9 %shard_map.121 = (f32[8,256]{1,0:T(8,128)}, f32[256,256]{1,0:T(8,128)}, f32[256,256]{1,0:T(8,128)}, f32[256,256]{1,0:T(8,128)}) custom-call(f32[8,256]{1,0:T(8,128)S(1)} %get-tuple-element.8.refs_0_, f32[256,256]{1,0:T(8,128)S(1)} %get-tuple-element.9.refs_1_, f32[256,256]{1,0:T(8,128)S(1)} %get-tuple-element.10.refs_2_, ...), custom_call_target="tpu_custom_call" | custom-call | tf_op jit(solution)/shard_map/pallas_call | solution.py:631

commit v8 on v7

--- a/solution.py
+++ b/solution.py
@@ -13,7 +13,7 @@
 HIGH = lax.Precision.HIGHEST
 MESH = pl.DeviceIdType.MESH
 ORDER = (2, 1, 3, 0)
-LOADS = (0, 4, 8, 12, 1, 5, 9, 13, 2, 6, 10, 14, 3, 7, 11, 15)
+LOADS = (0, 4, 8, 12, 2, 6, 10, 14, 1, 5, 9, 13, 3, 7, 11, 15)
 
 
 def transform_tables():
@@ -294,8 +294,7 @@
         pl.semaphore_wait(barrier, greetings)
     with jax.named_scope("spectrum_1"):
         to_partner(0)
-        products(1, 0, dsend)
-        to_partner(1)
+        products(0, 1, own)
     with jax.named_scope("row_halos"):
         for copy in borders:
             copy.wait()
@@ -314,7 +313,8 @@
             pl.when(inside)(copy.start)
             ns_copies.append((copy, inside))
     with jax.named_scope("spectrum_2"):
-        products(0, 1, own)
+        products(1, 0, dsend)
+        to_partner(1)
     with jax.named_scope("merge_0"):
         merge(0)
         for d in range(1, 4):
@@ -344,9 +344,6 @@
 
     with jax.named_scope("sum_y_0"):
         sum_y(0)
-
-    with jax.named_scope("sum_y_1"):
-        sum_y(1)
 
     with jax.named_scope("column_halos"):
         pl.when(row < 15)(ns_copies[0][0].wait_recv)
@@ -379,6 +376,9 @@
                 device_id=peer, device_id_type=MESH,
             )
             ew_copies.append((copy, inside))
+
+    with jax.named_scope("sum_y_1"):
+        sum_y(1)
 
     with jax.named_scope("far"):
         for at in range(2):

time: 25.9 us -> 25.7 us (level)
  the two profiles are of different devices: /device:TPU:1 before, /device:TPU:6 now
where the time goes in v8:
time: 25.7 us; the launch traced here: 25.6 us
  Pallas kernels  25 us (97%)
  between operations  0.64 us (2%)
    pallas_call x1, Pallas kernels, on_device(): pl.pallas_call(kernel, out_shape=shapes, in_specs=[pl.BlockSpec(memory_sp...  24 us
    pallas_call x1, Pallas kernels, on_device(): pl.pallas_call(write_out, out_shape=shapes, in_specs=[pl.BlockSpec(memory...  0.92 us

profile of v8, /device:TPU:6, one launch (start us, length us, event | category | flops | bytes accessed | tf_op | source)
XLA Modules:
  0.0 25.6 jit_solution(9870628690926664076)
XLA Ops:
  0.6 24.0 %shard_map.120 = (f32[8,256]{1,0:T(8,128)S(1)}, f32[256,256]{1,0:T(8,128)S(1)}, f32[256,256]{1,0:T(8,128)S(1)}, f32[256,256]{1,0:T(8,128)S(1)}) custom-call(bf16[1024,4096]{1,0:T(8,128)(2,1)} %bitcast.3, f32[32,128]{1,0:T(8,128)} %bitcast.4, f32[256,256]{1,0:T(8,128)} %speed.1, s32[256,256]{1,0:T(8,128)} %mask.1, s32[32,128]{1,0:T(8,128)} %bitcast.5, ...), custom_call_target="tpu_custom_call" | custom-call | tf_op jit(solution)/shard_map/pallas_call | solution.py:578
  24.7 0.9 %shard_map.121 = (f32[8,256]{1,0:T(8,128)}, f32[256,256]{1,0:T(8,128)}, f32[256,256]{1,0:T(8,128)}, f32[256,256]{1,0:T(8,128)}) custom-call(f32[8,256]{1,0:T(8,128)S(1)} %get-tuple-element.8.refs_0_, f32[256,256]{1,0:T(8,128)S(1)} %get-tuple-element.9.refs_1_, f32[256,256]{1,0:T(8,128)S(1)} %get-tuple-element.10.refs_2_, ...), custom_call_target="tpu_custom_call" | custom-call | tf_op jit(solution)/shard_map/pallas_call | solution.py:631

commit v9 on v8

--- a/solution.py
+++ b/solution.py
@@ -387,7 +387,7 @@
             pl.when(inside)(copy.start)
 
     with jax.named_scope("water_1"):
-        lax.fori_loop(3, 6, strip, 0)
+        lax.fori_loop(3, 7, strip, 0)
     with jax.named_scope("sum_x_0"):
         sum_x(0)
     with jax.named_scope("ghost_send"):
@@ -414,7 +414,7 @@
         sum_x(1)
 
     with jax.named_scope("more_water"):
-        lax.fori_loop(6, 9, lambda at, carry: strip(at % 8, carry), 0)
+        lax.fori_loop(7, 9, lambda at, carry: strip(at % 8, carry), 0)
 
     with jax.named_scope("selection"):
         @pl.when(is_edge)

time: 25.7 us -> 25.7 us (level)
  no operation moved by 1% of the time
where the time goes in v9:
time: 25.7 us; the launch traced here: 25.6 us
  Pallas kernels  25 us (97%)
  between operations  0.64 us (2%)
    pallas_call x1, Pallas kernels, on_device(): pl.pallas_call(kernel, out_shape=shapes, in_specs=[pl.BlockSpec(memory_sp...  24 us
    pallas_call x1, Pallas kernels, on_device(): pl.pallas_call(write_out, out_shape=shapes, in_specs=[pl.BlockSpec(memory...  0.92 us

profile of v9, /device:TPU:6, one launch (start us, length us, event | category | flops | bytes accessed | tf_op | source)
XLA Modules:
  0.0 25.6 jit_solution(11866097963782575608)
XLA Ops:
  0.6 24.0 %shard_map.120 = (f32[8,256]{1,0:T(8,128)S(1)}, f32[256,256]{1,0:T(8,128)S(1)}, f32[256,256]{1,0:T(8,128)S(1)}, f32[256,256]{1,0:T(8,128)S(1)}) custom-call(bf16[1024,4096]{1,0:T(8,128)(2,1)} %bitcast.3, f32[32,128]{1,0:T(8,128)} %bitcast.4, f32[256,256]{1,0:T(8,128)} %speed.1, s32[256,256]{1,0:T(8,128)} %mask.1, s32[32,128]{1,0:T(8,128)} %bitcast.5, ...), custom_call_target="tpu_custom_call" | custom-call | tf_op jit(solution)/shard_map/pallas_call | solution.py:578
  24.7 0.9 %shard_map.121 = (f32[8,256]{1,0:T(8,128)}, f32[256,256]{1,0:T(8,128)}, f32[256,256]{1,0:T(8,128)}, f32[256,256]{1,0:T(8,128)}) custom-call(f32[8,256]{1,0:T(8,128)S(1)} %get-tuple-element.8.refs_0_, f32[256,256]{1,0:T(8,128)S(1)} %get-tuple-element.9.refs_1_, f32[256,256]{1,0:T(8,128)S(1)} %get-tuple-element.10.refs_2_, ...), custom_call_target="tpu_custom_call" | custom-call | tf_op jit(solution)/shard_map/pallas_call | solution.py:631

commit v10 on v9

--- a/solution.py
+++ b/solution.py
@@ -12,7 +12,7 @@
 BF16 = jnp.bfloat16
 HIGH = lax.Precision.HIGHEST
 MESH = pl.DeviceIdType.MESH
-ORDER = (2, 1, 3, 0)
+ORDER = (1, 3, 2, 0)
 LOADS = (0, 4, 8, 12, 2, 6, 10, 14, 1, 5, 9, 13, 3, 7, 11, 15)
 
 
@@ -245,7 +245,7 @@
             for at in range(4):
                 xsend[part, at] = partial[at * 32 : at * 32 + 32]
             ahead(part, partial)
-            for d in (2, 1, 3):
+            for d in (1, 3, 2):
                 xcopy[part, d] = pltpu.make_async_remote_copy(
                     src_ref=xsend.at[part, (x + d) % 4], dst_ref=xrecv.at[part, d - 1],
                     send_sem=xsem.at[0, part, d - 1], recv_sem=xsem.at[1, part, d - 1],

time: 25.7 us -> 25.6 us (level)
  the two profiles are of different devices: /device:TPU:6 before, /device:TPU:1 now
where the time goes in v10:
time: 25.6 us; the launch traced here: 25.2 us
  Pallas kernels  24.5 us (96%)
  between operations  0.64 us (2%)
    pallas_call x1, Pallas kernels, on_device(): pl.pallas_call(kernel, out_shape=shapes, in_specs=[pl.BlockSpec(memory_sp...  23.6 us
    pallas_call x1, Pallas kernels, on_device(): pl.pallas_call(write_out, out_shape=shapes, in_specs=[pl.BlockSpec(memory...  0.92 us

profile of v10, /device:TPU:1, one launch (start us, length us, event | category | flops | bytes accessed | tf_op | source)
XLA Modules:
  0.0 25.2 jit_solution(9847157149965499163)
XLA Ops:
  0.6 23.6 %shard_map.120 = (f32[8,256]{1,0:T(8,128)S(1)}, f32[256,256]{1,0:T(8,128)S(1)}, f32[256,256]{1,0:T(8,128)S(1)}, f32[256,256]{1,0:T(8,128)S(1)}) custom-call(bf16[1024,4096]{1,0:T(8,128)(2,1)} %bitcast.3, f32[32,128]{1,0:T(8,128)} %bitcast.4, f32[256,256]{1,0:T(8,128)} %speed.1, s32[256,256]{1,0:T(8,128)} %mask.1, s32[32,128]{1,0:T(8,128)} %bitcast.5, ...), custom_call_target="tpu_custom_call" | custom-call | tf_op jit(solution)/shard_map/pallas_call | solution.py:578
  24.2 0.9 %shard_map.121 = (f32[8,256]{1,0:T(8,128)}, f32[256,256]{1,0:T(8,128)}, f32[256,256]{1,0:T(8,128)}, f32[256,256]{1,0:T(8,128)}) custom-call(f32[8,256]{1,0:T(8,128)S(1)} %get-tuple-element.8.refs_0_, f32[256,256]{1,0:T(8,128)S(1)} %get-tuple-element.9.refs_1_, f32[256,256]{1,0:T(8,128)S(1)} %get-tuple-element.10.refs_2_, ...), custom_call_target="tpu_custom_call" | custom-call | tf_op jit(solution)/shard_map/pallas_call | solution.py:631
